TPU v7x, 512 devices: a whole 4x4x16 slice. The times are simulated.
512 devices in a mesh: grp: 4 (over x), dom: 128 (over z, y, core).
Axes of the slice: x: 4, y: 4, z: 16, core: 2. Of those that a mesh axis runs over, the one named last changes fastest.
Arguments:
- node_state: float32 [65536, 6, 128], P(('grp', 'dom')), may hold values from -6 to 6
- node_dest: int32 [65536], P(('grp', 'dom')), may hold values from 0 to 127, as said below
- seg_nodes: float32 [6, 262144], P(None, ('grp', 'dom')), may hold values from -6 to 6
- seg_conn: int32 [3, 524288], P(None, ('grp', 'dom')), may hold values from 0 to 511
- pair_seg: int32 [512, 4, 32], P(('grp', 'dom')), may hold values from 0 to 7
- pair_slot: int32 [512, 4, 32], P(('grp', 'dom')), may hold values from 0 to 255, as said below
Outputs:
- node_force: float32 [65536, 3, 128], P(('grp', 'dom'))
Inputs may be any that keep to these rules, and one draw needn't show every extreme that they name: `node_dest`: at most 2 blocks of one device name the same contact domain; in every grp row one contact domain receives exactly 2 blocks from every device of that row; every device sends at least one block to the contact domain of its own dom index. `pair_slot`: every entry names a slot d * 2 + k that holds a block: device (r, d) sends more than k blocks to the contact domain.
All inputs are finite; a program needn't handle non-finite values.
Results may differ from a plain program's by a relative error of at most 0.00023.
Values sent between devices are 32-bit elements; how exact they have to be, the bound alone decides.
No kernel may reach another device: no remote copies, remote signals or barrier semaphores. Data moves between devices by JAX's collectives and lax.ppermute only.
A program may use at most 64 MiB of HBM per device.

v0:
```python
import jax
import jax.numpy as jnp
from jax import lax
from jax.sharding import Mesh
from jax.sharding import PartitionSpec as P

SEG_BLK = 128
DOM = ("dom_0", "dom_1", "dom_2")
GRP_DOM = ("grp", "dom_0", "dom_1", "dom_2")


time_step = 0.5
stiffness = 0.5
radius_sq = 0.5


def in_blocks(shard, dim, devices):
    dims = shard.shape
    blocks = shard.reshape(*dims[:dim], devices, dims[dim] // devices, *dims[dim + 1 :])
    return jnp.moveaxis(blocks, dim, 0)


def in_order(blocks, dim):
    blocks = jnp.moveaxis(blocks, 0, dim)
    dims = blocks.shape
    return blocks.reshape(*dims[:dim], dims[dim] * dims[dim + 1], *dims[dim + 2 :])


def moved_by_axis(blocks, axes, turns):
    dims = [lax.axis_size(a) for a in axes]
    blocks = blocks.reshape(*dims, *blocks.shape[1:])
    for k in turns:
        blocks = lax.all_to_all(blocks, axes[k], split_axis=k, concat_axis=k, tiled=True)
    return blocks.reshape(-1, *blocks.shape[len(axes) :])


def two_step_exchange(shard, groups, turns, split_dim, concat_dim):
    devices = lax.axis_size(groups[0]) * lax.axis_size(groups[1])
    blocks = in_blocks(shard, split_dim, devices)
    return in_order(moved_by_axis(blocks, groups, turns), concat_dim)


def seg_geometry(corners):
    corner_a = corners[:, 0]
    corner_b = corners[:, 1]
    corner_c = corners[:, 2]
    edge_one = corner_b[0:3] - corner_a[0:3]
    edge_two = corner_c[0:3] - corner_a[0:3]
    normal = 0.5 * jnp.stack(
        [
            edge_one[1] * edge_two[2] - edge_one[2] * edge_two[1],
            edge_one[2] * edge_two[0] - edge_one[0] * edge_two[2],
            edge_one[0] * edge_two[1] - edge_one[1] * edge_two[0],
        ]
    )
    centre = (corner_a[0:3] + corner_b[0:3] + corner_c[0:3]) / 3.0
    motion = (corner_a[3:6] + corner_b[3:6] + corner_c[3:6]) / 3.0
    return jnp.concatenate([normal, centre, motion], axis=0)


def tile_force(node_rows, geometry):
    clearance = jnp.zeros((geometry.shape[1], node_rows.shape[1]), jnp.float32)
    distance = jnp.zeros((geometry.shape[1], node_rows.shape[1]), jnp.float32)
    for axis_id in range(3):
        offset = node_rows[axis_id][None, :] - geometry[3 + axis_id][:, None]
        drift = node_rows[3 + axis_id][None, :] - geometry[6 + axis_id][:, None]
        clearance = clearance + geometry[axis_id][:, None] * (offset + time_step * drift)
        distance = distance + offset * offset
    pressure = stiffness * jnp.exp(-distance / radius_sq) * jnp.maximum(-clearance, 0.0)
    return jnp.dot(
        geometry[0:3], pressure, precision=lax.Precision.HIGHEST, preferred_element_type=jnp.float32
    )


def place_rows(slot_ids, values, slot_total):
    onehot = (slot_ids[None, :] == jnp.arange(slot_total, dtype=jnp.int32)[:, None]).astype(
        jnp.float32
    )
    flattened = values.reshape(values.shape[0], -1)
    placed = jnp.dot(
        onehot, flattened, precision=lax.Precision.HIGHEST, preferred_element_type=jnp.float32
    )
    return placed.reshape((slot_total,) + values.shape[1:])


def shards(node_state, node_dest, seg_nodes, seg_conn, pair_seg, pair_slot):
    dom_count = lax.axis_size(DOM)
    grp_count = lax.axis_size("grp")
    block_count = node_state.shape[0]
    capacity = max(2, 2 * block_count // dom_count)
    slot_count = dom_count * capacity
    order_ids = jnp.arange(block_count, dtype=jnp.int32)
    earlier = order_ids[None, :] < order_ids[:, None]
    same_dom = node_dest[:, None] == node_dest[None, :]
    slot_rank = jnp.sum((same_dom & earlier).astype(jnp.int32), axis=1)
    target_slot = node_dest * capacity + slot_rank
    outgoing = place_rows(target_slot, node_state, slot_count)
    received = two_step_exchange(outgoing, (("dom_0", "dom_1"), "dom_2"), (1, 0), 0, 0)
    corners = jnp.take(seg_nodes, seg_conn, axis=1)
    geometry = seg_geometry(corners)
    seg_blocks = geometry.shape[1] // SEG_BLK
    geo_blocks = jnp.transpose(geometry.reshape(9, seg_blocks, SEG_BLK), (1, 0, 2))
    seg_table = pair_seg[0]
    slot_table = pair_slot[0]
    geo_all = lax.all_gather(geo_blocks, "grp", axis=0, tiled=True)
    seg_in, slot_in = (
        lax.all_to_all(seg_table, "grp", split_axis=0, concat_axis=0, tiled=True),
        lax.all_to_all(slot_table, "grp", split_axis=0, concat_axis=0, tiled=True),
    )
    owner_base = (jnp.arange(grp_count, dtype=jnp.int32) * seg_blocks)[:, None]
    seg_ids = (seg_in + owner_base).reshape(-1)
    slot_ids = slot_in.reshape(-1)
    forces = jax.vmap(tile_force)(
        jnp.take(received, slot_ids, axis=0), jnp.take(geo_all, seg_ids, axis=0)
    )
    own_forces = place_rows(slot_ids, forces, slot_count)
    returned = lax.all_to_all(own_forces, DOM, split_axis=0, concat_axis=0, tiled=True)
    return jnp.take(returned, target_slot, axis=0)


def solution(mesh):
    split = Mesh(
        mesh.devices.reshape(mesh.shape["grp"], 16, 4, 2), ("grp", "dom_0", "dom_1", "dom_2")
    )
    placed = (
        P(GRP_DOM, None, None),
        P(GRP_DOM),
        P(None, GRP_DOM),
        P(None, GRP_DOM),
        P(GRP_DOM, None, None),
        P(GRP_DOM, None, None),
    )
    return jax.shard_map(
        shards, mesh=split, in_specs=placed, out_specs=P(GRP_DOM, None, None), check_vma=False
    )
```

profile of v0, /device:TPU:1, one launch (start us, length us, event | category | flops | bytes accessed | tf_op | source)
XLA Modules:
  0.0 166.9 jit_solution(1052670801400604042)
XLA Ops:
  0.0 0.9 convert_reduce_fusion
  0.9 0.7 compare_and_fusion.3
  1.6 1.2 copy.65
  2.8 0.5 fusion.34
  3.3 10.8 %all_to_all.39 = f32[64,2,2,6,128]{4,0,3,2,1:T(8,128)S(1)} all-to-all(f32[64,2,2,6,128]{4,0,3,2,1:T(8,128)S(1)} %fusion.34), channel_id=1, replica_groups=mesh['grp'=4,'dom_0'=16,'dom_1'=4,'dom_2'=2] {'dom_2'}, dimensions={1} | all-to-all | bytes 1572864 | tf_op jit(solution)/shard_map/all_to_all | solution.py:33
  14.1 3.2 %all-to-all-start.1 = ((s32[4,1,32]{2,1,0:T(1,128)}), s32[4,1,32]{2,1,0:T(1,128)S(1)}, u32[]{:S(2)}, u32[]{:S(2)}) async-start(s32[4,1,32]{2,1,0:T(1,128)} %bitcast.4), calls=%async_computation.1 | async-start | bytes 4096 | tf_op jit(solution)/shard_map/all_to_all | solution.py:107
  17.4 4.0 %all-to-all-done.1 = s32[4,1,32]{2,1,0:T(1,128)S(1)} async-done(((s32[4,1,32]{2,1,0:T(1,128)}), s32[4,1,32]{2,1,0:T(1,128)S(1)}, u32[]{:S(2)}, u32[]{:S(2)}) %all-to-all-start.1) | async-done | bytes 544 | tf_op jit(solution)/shard_map/all_to_all | solution.py:107
  21.4 3.2 %all-to-all-start = ((s32[4,1,32]{2,1,0:T(1,128)}), s32[4,1,32]{2,1,0:T(1,128)S(1)}, u32[]{:S(2)}, u32[]{:S(2)}) async-start(s32[4,1,32]{2,1,0:T(1,128)} %bitcast.1), calls=%async_computation | async-start | bytes 4096 | tf_op jit(solution)/shard_map/all_to_all | solution.py:108
  24.6 1.5 copy.66
  26.1 2.5 %all-to-all-done = s32[4,1,32]{2,1,0:T(1,128)S(1)} async-done(((s32[4,1,32]{2,1,0:T(1,128)}), s32[4,1,32]{2,1,0:T(1,128)S(1)}, u32[]{:S(2)}, u32[]{:S(2)}) %all-to-all-start) | async-done | bytes 544 | tf_op jit(solution)/shard_map/all_to_all | solution.py:108
  28.6 13.9 %all-to-all-start.3 = ((f32[64,2,2,6,128]{4,2,3,1,0:T(2,128)}), f32[64,2,2,6,128]{4,2,3,1,0:T(2,128)S(1)}, u32[]{:S(2)}, u32[]{:S(2)}) async-start(f32[64,2,2,6,128]{4,2,3,1,0:T(2,128)} %copy.66), calls=%async_computation.3 | async-start | bytes 1572864 | tf_op jit(solution)/shard_map/all_to_all | solution.py:33
  43.0 8.1 %gather_fusion = f32[3072,6]{1,0:T(8,128)S(1)} fusion(f32[6,512]{0,1:T(8,128)S(1)} %copy.62, s32[3072]{0:T(1024)S(1)} %broadcast_clamp_fusion), kind=kCustom, calls=%fused_computation | custom fusion | bytes 159744 | tf_op jit(solution)/shard_map/jit(_take)/gather | solution.py:99
  51.1 0.5 copy.63
  51.7 10.0 %all_gather.3 = f32[32,9,128]{2,0,1:T(8,128)S(1)} all-gather(f32[8,9,128]{2,0,1:T(8,128)S(1)} %maximum_bitcast_fusion), channel_id=1, replica_groups=mesh['grp'=4,'dom_0'=16,'dom_1'=4,'dom_2'=2] {'grp'}, dimensions={0}, use_global_device_ids=true | all-gather | bytes 184320 | tf_op jit(solution)/shard_map/all_gather | solution.py:105
  61.9 0.5 broadcast.150
  62.4 0.7 reduce.10
  63.3 0.7 reduce.11
  64.0 0.8 gather_fusion.1
  64.9 0.2 broadcast_select_fusion
  65.1 0.4 fusion.54
  65.5 15.7 %all-to-all-done.3 = f32[64,2,2,6,128]{4,2,3,1,0:T(2,128)S(1)} async-done(((f32[64,2,2,6,128]{4,2,3,1,0:T(2,128)}), f32[64,2,2,6,128]{4,2,3,1,0:T(2,128)S(1)}, u32[]{:S(2)}, u32[]{:S(2)}) %all-to-all-start.3) | async-done | bytes 786464 | tf_op jit(solution)/shard_map/all_to_all | solution.py:33
  81.2 0.3 copy.67
  81.4 0.5 copy.68
  81.9 0.8 gather_fusion.2
  82.9 0.3 fusion.55
  83.2 37.2 %fusion.14 = f32[128,3,128]{2,1,0:T(4,128)S(1)} fusion(f32[128,128]{1,0:T(8,128)S(1)} %bitcast.77, f32[128,128]{1,0:T(8,128)S(1)} %bitcast.86, f32[128,128]{1,0:T(8,128)S(1)} %bitcast.78, f32[128,128]{1,0:T(8,128)S(1)} %bitcast.79, f32[128,128]{1,0:T(8,128)S(1)} %bitcast.87, f32[128,128]{1,0:T(8,128)S(1)} %bitcast.80, f32[128,128]{1,0:T(8,128)S(1)} %bitcast.81, ...), kind=kOutput, calls=%fused_computation.24 | convolution fusion | flops 134217728 | bytes 1441792 | tf_op jit(solution)/shard_map/vmap()/dot_general | solution.py:70
  120.5 0.3 fusion.37
  120.9 1.1 copy.70
  122.0 12.6 %all-to-all-start.4 = ((f32[256,3,128]{2,1,0:T(4,128)}), f32[256,3,128]{2,1,0:T(4,128)S(1)}, u32[]{:S(2)}, u32[]{:S(2)}) async-start(f32[256,3,128]{2,1,0:T(4,128)} %copy.70), calls=%async_computation.4 | async-start | bytes 1048576 | tf_op jit(solution)/shard_map/all_to_all | solution.py:117
  134.6 30.7 %all-to-all-done.4 = f32[256,3,128]{2,1,0:T(4,128)S(1)} async-done(((f32[256,3,128]{2,1,0:T(4,128)}), f32[256,3,128]{2,1,0:T(4,128)S(1)}, u32[]{:S(2)}, u32[]{:S(2)}) %all-to-all-start.4) | async-done | bytes 393248 | tf_op jit(solution)/shard_map/all_to_all | solution.py:117
  165.2 0.8 gather_fusion.3
  166.2 0.7 copy.71
  (36 shorter events, 1.6 us)
Async XLA Ops:
  2.7 14.6 %copy-start = (s32[3,1024]{1,0:T(4,128)S(1)}, s32[3,1024]{1,0:T(4,128)}, u32[]{:S(2)}) copy-start(s32[3,1024]{1,0:T(4,128)} %param.9) | copy-start | bytes 36868
  14.1 7.3 %all-to-all-start.1 = ((s32[4,1,32]{2,1,0:T(1,128)}), s32[4,1,32]{2,1,0:T(1,128)S(1)}, u32[]{:S(2)}, u32[]{:S(2)}) async-start(s32[4,1,32]{2,1,0:T(1,128)} %bitcast.4), calls=%async_computation.1 | async-start | bytes 4096 | tf_op jit(solution)/shard_map/all_to_all | solution.py:107
  21.4 7.3 %all-to-all-start = ((s32[4,1,32]{2,1,0:T(1,128)}), s32[4,1,32]{2,1,0:T(1,128)S(1)}, u32[]{:S(2)}, u32[]{:S(2)}) async-start(s32[4,1,32]{2,1,0:T(1,128)} %bitcast.1), calls=%async_computation | async-start | bytes 4096 | tf_op jit(solution)/shard_map/all_to_all | solution.py:108
  24.6 18.2 %copy-start.1 = (f32[6,512]{1,0:T(8,128)S(1)}, f32[6,512]{1,0:T(8,128)}, u32[]{:S(2)}) copy-start(f32[6,512]{1,0:T(8,128)} %param.8) | copy-start | bytes 36868
  28.6 52.5 %all-to-all-start.3 = ((f32[64,2,2,6,128]{4,2,3,1,0:T(2,128)}), f32[64,2,2,6,128]{4,2,3,1,0:T(2,128)S(1)}, u32[]{:S(2)}, u32[]{:S(2)}) async-start(f32[64,2,2,6,128]{4,2,3,1,0:T(2,128)} %copy.66), calls=%async_computation.3 | async-start | bytes 1572864 | tf_op jit(solution)/shard_map/all_to_all | solution.py:33
  122.0 43.3 %all-to-all-start.4 = ((f32[256,3,128]{2,1,0:T(4,128)}), f32[256,3,128]{2,1,0:T(4,128)S(1)}, u32[]{:S(2)}, u32[]{:S(2)}) async-start(f32[256,3,128]{2,1,0:T(4,128)} %copy.70), calls=%async_computation.4 | async-start | bytes 1048576 | tf_op jit(solution)/shard_map/all_to_all | solution.py:117
where the time goes:
time: 169 us; the launch traced here: 167 us
  waiting for transfers between devices  52.8 us (31%)
  matrix products  38.1 us (23%)
  starting transfers between devices  32.9 us (19%)
  blocking collectives  20.9 us (12%)
  local copies, waits for them, and re-layouts  18.2 us (11%)
  other arithmetic  3.67 us (2%)
    dot_general x1, matrix products, tile_force(): jnp.dot(geometry[0:3], pressure, precision=lax.Precision.HIGHEST, preferr...  37.2 us
    all_to_all x1, waiting for transfers between devices, shards(): lax.all_to_all(own_forces, DOM, split_axis=0, concat_axis=0, tiled=True)  30.7 us
    all_to_all x1, waiting for transfers between devices, moved_by_axis(): lax.all_to_all(blocks, axes[k], split_axis=k, concat_axis=k, tiled=True)  15.7 us
    all_to_all x1, starting transfers between devices, moved_by_axis(): lax.all_to_all(blocks, axes[k], split_axis=k, concat_axis=k, tiled=True)  13.9 us
    all_to_all x1, starting transfers between devices, shards(): lax.all_to_all(own_forces, DOM, split_axis=0, concat_axis=0, tiled=True)  12.6 us
    all_to_all x1, blocking collectives, moved_by_axis(): lax.all_to_all(blocks, axes[k], split_axis=k, concat_axis=k, tiled=True)  10.8 us
    all_gather x1, blocking collectives, shards(): geo_all = lax.all_gather(geo_blocks, 'grp', axis=0, tiled=True)  10 us
    gather x2, local copies, waits for them, and re-layouts, shards(): corners = jnp.take(seg_nodes, seg_conn, axis=1)  8.59 us
  transfers between devices with their start and end apart: 4, of which 4 were waited for; matrix products, arithmetic and copies ran while one was open for 8% of the time, Pallas kernels for 0%

commit v1 on v0

v1 whole, which is shorter than its diff:
```python
import functools
import math

import jax
import jax.numpy as jnp
from jax import lax
from jax.experimental import pallas as pl
from jax.experimental.pallas import tpu as pltpu
from jax.sharding import Mesh
from jax.sharding import PartitionSpec as P

BLK = 128
COPIES = 4
TIME_STEP = 0.5
STIFFNESS = 0.5
RADIUS_SQ = 0.5
SCALE = math.sqrt(math.log2(math.e) / RADIUS_SQ)
GRP_DOM = ("grp", "zh", "zl", "y", "core")
NEAR = ("zl", "y", "core")
VMEM = pl.BlockSpec(memory_space=pltpu.VMEM)
SMEM = pl.BlockSpec(memory_space=pltpu.SMEM)


def lane_pick(row, index):
    return jnp.take_along_axis(row, index, axis=1, mode="promise_in_bounds")


def geometry_kernel(nodes_ref, conn_ref, seg_ref, slot_ref, out_ref):
    blocks = conn_ref.shape[1] // BLK
    parts = nodes_ref.shape[1] // BLK
    index = [
        jnp.concatenate([conn_ref[k : k + 1, b * BLK : (b + 1) * BLK] for b in range(blocks)], axis=0)
        for k in range(3)
    ]
    lanes = [i & (BLK - 1) for i in index]
    part = [i >> 7 for i in index]
    corner = [[None] * 6 for _ in range(3)]
    for comp in range(6):
        for p in range(parts):
            row = jnp.broadcast_to(nodes_ref[comp : comp + 1, p * BLK : (p + 1) * BLK], (blocks, BLK))
            for k in range(3):
                got = lane_pick(row, lanes[k])
                corner[k][comp] = got if p == 0 else jnp.where(part[k] == p, got, corner[k][comp])
    a, b, c = corner
    e = [b[i] - a[i] for i in range(3)]
    f = [c[i] - a[i] for i in range(3)]
    n = [
        0.5 * (e[1] * f[2] - e[2] * f[1]),
        0.5 * (e[2] * f[0] - e[0] * f[2]),
        0.5 * (e[0] * f[1] - e[1] * f[0]),
    ]
    m = [(a[i] + b[i] + c[i]) / 3.0 for i in range(3)]
    u = [(a[i] + b[i] + c[i]) / 3.0 for i in range(3, 6)]
    s = sum(n[i] * (m[i] + TIME_STEP * u[i]) for i in range(3))
    rows = n + [m[i] * SCALE for i in range(3)] + [s]
    tables = jnp.concatenate(
        [slot_ref[...], seg_ref[...], jnp.zeros((blocks - 2, BLK), jnp.int32)], axis=0
    ).astype(jnp.float32)
    for copy in range(out_ref.shape[0]):
        for i, row in enumerate(rows + [tables]):
            out_ref[copy, :, i, :] = row


def three_parts(x):
    high = x.astype(jnp.bfloat16)
    rest = x - high.astype(jnp.float32)
    mid = rest.astype(jnp.bfloat16)
    low = (rest - mid.astype(jnp.float32)).astype(jnp.bfloat16)
    return high, mid, low


def exact_dot(onehot, x):
    return sum(jnp.dot(onehot, part, preferred_element_type=jnp.float32) for part in three_parts(x))


def place_kernel(copies, near, dest_ref, nodes_ref, out_ref, pick_ref):
    blocks = dest_ref.shape[1]
    slots = near * copies * 2
    across = jnp.broadcast_to(dest_ref[...].astype(jnp.float32), (blocks, blocks))
    down = across.T
    i = lax.broadcasted_iota(jnp.int32, (blocks, blocks), 0)
    j = lax.broadcasted_iota(jnp.int32, (blocks, blocks), 1)
    same = across == down

    def slot_of(dest, rank):
        dest = dest.astype(jnp.int32)
        return ((dest & (near - 1)) * copies + lax.div(dest, near)) * 2 + rank.astype(jnp.int32)

    rank_row = jnp.sum(jnp.where(same & (i < j), 1.0, 0.0), axis=0, keepdims=True)
    slot_row = slot_of(dest_ref[...], rank_row)
    onehot = (lax.broadcasted_iota(jnp.int32, (slots, blocks), 0) == slot_row).astype(jnp.float32).astype(jnp.bfloat16)
    rank_col = jnp.sum(jnp.where(same & (j < i), 1.0, 0.0), axis=1, keepdims=True)
    slot_col = slot_of(down[:, 0:1], rank_col)
    pick_ref[...] = (
        (lax.broadcasted_iota(jnp.int32, (blocks, slots), 1) == slot_col).astype(jnp.float32).astype(jnp.bfloat16)
    )
    for comp in range(6):
        x = nodes_ref[comp % 3]
        row = x * SCALE if comp < 3 else x + TIME_STEP * nodes_ref[comp]
        out_ref[:, comp] = exact_dot(onehot, row).reshape(near, copies * 2, BLK)


def force_kernel(codes_ref, geo_ref, nodes_ref, out_ref, turned, todo):
    near, _, slots, _ = out_ref.shape
    pairs = codes_ref.shape[0]
    for t in range(turned.shape[0]):
        turned[t] = geo_ref[t * BLK : (t + 1) * BLK, :].T
    out_ref[...] = jnp.zeros_like(out_ref)

    def keep(k, count):
        code = codes_ref[k]
        todo[count] = code
        return count + jnp.where(code >= 0, 1, 0)

    count = lax.fori_loop(0, pairs, keep, jnp.int32(0), unroll=8)

    def pair(k, _):
        code = todo[k]
        source = code & 63
        slot = (code >> 6) & 31
        block = code >> 11
        tile = block >> 4
        lane = (block & 15) * 8
        row = [nodes_ref[source, comp, pl.ds(slot, 1), :] for comp in range(6)]
        x = [jnp.broadcast_to(r, (8, BLK)) for r in row]
        index = [jnp.full((8, BLK), lane + q, jnp.int32) for q in range(7)]
        force = [jnp.zeros((8, BLK), jnp.float32)] * 3
        for g in range(BLK // 8):
            seg = turned[tile, g * 8 : (g + 1) * 8, :]
            q = [lane_pick(seg, index[i]) for i in range(7)]
            d = [x[i] - q[3 + i] for i in range(3)]
            close = q[6] - (q[0] * x[3] + q[1] * x[4] + q[2] * x[5])
            far = d[0] * d[0] + d[1] * d[1] + d[2] * d[2]
            pressure = jnp.exp2(-far) * jnp.maximum(close, 0.0)
            force = [force[i] + q[i] * pressure for i in range(3)]
        for i in range(3):
            at = (source, i, pl.ds(slot, 1), slice(None))
            out_ref[at] = out_ref[at] + jnp.sum(force[i], axis=0, keepdims=True)
        return 0

    lax.fori_loop(0, count, pair, 0)


def pick_kernel(pick_ref, back_ref, out_ref):
    for comp in range(3):
        rows = back_ref[:, comp].reshape(pick_ref.shape[1], BLK)
        out_ref[comp] = STIFFNESS * exact_dot(pick_ref[...], rows)


def f32(*shape):
    return jax.ShapeDtypeStruct(shape, jnp.float32)


def shards(node_state, node_dest, seg_nodes, seg_conn, pair_seg, pair_slot):
    groups = lax.axis_size("grp")
    copies = lax.axis_size("zh")
    near = lax.axis_size(NEAR)
    blocks = node_state.shape[0]
    seg_blocks = seg_conn.shape[1] // BLK
    per_group = pair_seg.shape[2]
    slots = copies * 2

    geometry = pl.pallas_call(
        geometry_kernel, out_shape=f32(copies, seg_blocks, 8, BLK), in_specs=[VMEM] * 4, out_specs=VMEM
    )(seg_nodes, seg_conn, pair_seg.reshape(1, BLK), pair_slot.reshape(1, BLK))
    geometry = geometry.reshape(copies, seg_blocks * 8, BLK)
    geometry = lax.all_to_all(geometry, "zh", split_axis=0, concat_axis=0, tiled=True)
    geometry = jnp.broadcast_to(
        geometry.reshape(1, copies * seg_blocks * 8, BLK), (groups, copies * seg_blocks * 8, BLK)
    )
    geometry = lax.all_to_all(geometry, "grp", split_axis=0, concat_axis=0, tiled=True)

    outgoing, pick = pl.pallas_call(
        functools.partial(place_kernel, copies, near),
        out_shape=(f32(near, 6, slots, BLK), jax.ShapeDtypeStruct((blocks, near * slots), jnp.bfloat16)),
        in_specs=[VMEM] * 2,
        out_specs=[VMEM] * 2,
    )(node_dest.reshape(1, blocks), jnp.transpose(node_state, (1, 0, 2)))
    received = lax.all_to_all(
        outgoing.reshape(near, 6 * slots, BLK), NEAR, split_axis=0, concat_axis=0, tiled=True
    ).reshape(near, 6, slots, BLK)

    tables = geometry.reshape(groups, copies, seg_blocks, 8, BLK)[:, :, 0:2, 7, :].reshape(
        groups * copies, 2, groups, per_group
    )
    tables = lax.dynamic_index_in_dim(tables, lax.axis_index("grp"), axis=2, keepdims=False).astype(jnp.int32)
    slot, seg = tables[:, 0], tables[:, 1]
    owner = jnp.arange(groups * copies, dtype=jnp.int32)[:, None]
    source = slot // 2
    place = (owner % copies) * 2 + slot % 2
    block = owner * seg_blocks + seg
    codes = (source % near) + place * 64 + block * 2048
    codes = jnp.where(source // near == lax.axis_index("zh"), codes, -1).reshape(-1)

    tiles = groups * copies * seg_blocks * 8 // BLK
    forces = pl.pallas_call(
        force_kernel,
        out_shape=f32(near, 3, slots, BLK),
        in_specs=[SMEM, VMEM, VMEM],
        out_specs=VMEM,
        scratch_shapes=[
            pltpu.VMEM((tiles, BLK, BLK), jnp.float32),
            pltpu.SMEM((codes.shape[0] + 1,), jnp.int32),
        ],
    )(codes, geometry.reshape(tiles * BLK, BLK), received)
    back = lax.all_to_all(
        forces.reshape(near, 3 * slots, BLK), NEAR, split_axis=0, concat_axis=0, tiled=True
    ).reshape(near, 3, slots, BLK)
    out = pl.pallas_call(pick_kernel, out_shape=f32(3, blocks, BLK), in_specs=[VMEM] * 2, out_specs=VMEM)(pick, back)
    return jnp.transpose(out, (1, 0, 2))


def solution(mesh):
    groups = mesh.shape["grp"]
    split = Mesh(mesh.devices.reshape(groups, COPIES, 16 // COPIES, 4, 2), GRP_DOM)
    placed = (
        P(GRP_DOM, None, None),
        P(GRP_DOM),
        P(None, GRP_DOM),
        P(None, GRP_DOM),
        P(GRP_DOM, None, None),
        P(GRP_DOM, None, None),
    )
    return jax.shard_map(
        shards, mesh=split, in_specs=placed, out_specs=P(GRP_DOM, None, None), check_vma=False
    )
```

time: 169 us -> 160 us (0.947)
  Pallas kernels: 0 us -> 62.2 us
  matrix products: 38.1 us -> 0 us
  blocking collectives: 20.9 us -> 52.2 us
  waiting for transfers between devices: 52.8 us -> 24.7 us
  starting transfers between devices: 32.9 us -> 14.5 us
  local copies, waits for them, and re-layouts: 18.2 us -> 4.29 us
  other arithmetic: 3.67 us -> 0.64 us
    pallas_call x0 -> x4, Pallas kernels: none -> 62.2 us  [the longest x1 56 us: shards(): pl.pallas_call(force_kernel, out_shape=f32(near, 3, slots, BLK), in_specs...]
    all_to_all x1 -> x2, blocking collectives: 10.8 us -> 52.2 us  [the longest x1 28.3 us: shards(): lax.all_to_all(geometry, 'zh', split_axis=0, concat_axis=0, tiled=True)]
    dot_general x3 -> x0, matrix products: 38.1 us -> none  [the longest x1 37.2 us: tile_force(): jnp.dot(geometry[0:3], pressure, precision=lax.Precision.HIGHEST, preferr...]
    all_to_all x4 -> x2, waiting for transfers between devices: 52.8 us -> 24.7 us  [the longest x1 20.3 us: shards(): lax.all_to_all(outgoing.reshape(near, 6 * slots, BLK), NEAR, split_axis=0...]
    all_to_all x4 -> x2, starting transfers between devices: 32.9 us -> 14.5 us  [the longest x1 10.5 us: shards(): lax.all_to_all(outgoing.reshape(near, 6 * slots, BLK), NEAR, split_axis=0...]
    gather x5 -> x0, local copies, waits for them, and re-layouts: 10.9 us -> none  [the longest x2 8.59 us: shards(): corners = jnp.take(seg_nodes, seg_conn, axis=1)]
    all_gather x1 -> x0, blocking collectives: 10 us -> none  [shards(): geo_all = lax.all_gather(geo_blocks, 'grp', axis=0, tiled=True)]
    all_to_all x5 -> x0, local copies, waits for them, and re-layouts: 2.44 us -> none  [the longest x2 1.76 us: moved_by_axis(): lax.all_to_all(blocks, axes[k], split_axis=k, concat_axis=k, tiled=True)]
  transfers between devices with their start and end apart: 4 -> 2, of which waited for: 4 -> 2; matrix products, arithmetic and copies ran while one was open for 8% -> 1% of each run, Pallas kernels for 0% -> 2%
where the time goes in v1:
time: 160 us; the launch traced here: 159 us
  Pallas kernels  62.2 us (39%)
  blocking collectives  52.2 us (33%)
  waiting for transfers between devices  24.7 us (15%)
  starting transfers between devices  14.5 us (9%)
  local copies, waits for them, and re-layouts  4.29 us (3%)
    pallas_call x1, Pallas kernels, shards(): pl.pallas_call(force_kernel, out_shape=f32(near, 3, slots, BLK), in_specs...  56 us
    all_to_all x1, blocking collectives, shards(): lax.all_to_all(geometry, 'zh', split_axis=0, concat_axis=0, tiled=True)  28.3 us
    all_to_all x1, blocking collectives, shards(): lax.all_to_all(forces.reshape(near, 3 * slots, BLK), NEAR, split_axis=0,...  23.9 us
    all_to_all x1, waiting for transfers between devices, shards(): lax.all_to_all(outgoing.reshape(near, 6 * slots, BLK), NEAR, split_axis=0...  20.3 us
    all_to_all x1, starting transfers between devices, shards(): lax.all_to_all(outgoing.reshape(near, 6 * slots, BLK), NEAR, split_axis=0...  10.5 us
    all_to_all x1, waiting for transfers between devices, shards(): lax.all_to_all(geometry, 'grp', split_axis=0, concat_axis=0, tiled=True)  4.46 us
    all_to_all x1, starting transfers between devices, shards(): lax.all_to_all(geometry, 'grp', split_axis=0, concat_axis=0, tiled=True)  4.01 us
  transfers between devices with their start and end apart: 2, of which 2 were waited for; matrix products, arithmetic and copies ran while one was open for 1% of the time, Pallas kernels for 2%

profile of v1, /device:TPU:1, one launch (start us, length us, event | category | flops | bytes accessed | tf_op | source)
XLA Modules:
  0.0 158.5 jit_solution(3163430251356444827)
XLA Ops:
  0.0 0.0 copy-start.2
  0.0 1.3 reshape.61.seg_ref
  1.3 0.0 copy-done.2
  1.3 0.6 reshape.62.slot_ref
  1.9 1.7 %shard_map.65 = f32[4,8,8,128]{3,2,1,0:T(8,128)} custom-call(f32[6,512]{1,0:T(8,128)} %nodes_ref.1, s32[3,1024]{1,0:T(4,128)} %conn_ref.1, s32[1,128]{1,0:T(1,128)} %reshape.61.seg_ref, s32[1,128]{1,0:T(1,128)} %reshape.62.slot_ref), custom_call_target="tpu_custom_call" | custom-call | tf_op jit(solution)/shard_map/pallas_call | solution.py:163
  3.6 28.3 %all_to_all.20 = f32[4,64,128]{2,1,0:T(8,128)S(1)} all-to-all(f32[4,64,128]{2,1,0:T(8,128)} %bitcast.19), channel_id=1, replica_groups=mesh['grp'=4,'zh'=4,'zl'=4,'y'=4,'core'=2] {'zh'}, dimensions={0} | all-to-all | bytes 262144 | tf_op jit(solution)/shard_map/all_to_all | solution.py:167
  31.8 0.8 broadcast_in_dim.11
  32.7 4.0 %all-to-all-start.1 = ((f32[4,256,128]{2,1,0:T(8,128)}), f32[4,256,128]{2,1,0:T(8,128)S(1)}, u32[]{:S(2)}, u32[]{:S(2)}) async-start(f32[4,256,128]{2,1,0:T(8,128)} %broadcast_in_dim.11), calls=%async_computation.1 | async-start | bytes 1048576 | tf_op jit(solution)/shard_map/all_to_all | solution.py:171
  36.7 2.5 %shard_map.64 = (f32[32,6,8,128]{3,2,1,0:T(8,128)}, bf16[128,256]{1,0:T(8,128)(2,1)}) custom-call(s32[1,128]{1,0:T(1,128)} %bitcast.22, f32[6,128,128]{2,1,0:T(8,128)} %bitcast.20), custom_call_target="tpu_custom_call" | custom-call | tf_op jit(solution)/shard_map/pallas_call | solution.py:173
  39.2 4.5 %all-to-all-done.1 = f32[4,256,128]{2,1,0:T(8,128)S(1)} async-done(((f32[4,256,128]{2,1,0:T(8,128)}), f32[4,256,128]{2,1,0:T(8,128)S(1)}, u32[]{:S(2)}, u32[]{:S(2)}) %all-to-all-start.1) | async-done | bytes 524320 | tf_op jit(solution)/shard_map/all_to_all | solution.py:171
  43.6 0.0 copy-start.1
  43.6 10.5 %all-to-all-start.2 = ((f32[32,48,128]{2,1,0:T(8,128)}), f32[32,48,128]{2,1,0:T(8,128)S(1)}, u32[]{:S(2)}, u32[]{:S(2)}) async-start(f32[32,48,128]{2,1,0:T(8,128)} %bitcast.17), calls=%async_computation.2 | async-start | bytes 1572864 | tf_op jit(solution)/shard_map/all_to_all | solution.py:179
  54.1 0.1 add.64
  54.2 0.1 add.65
  54.3 0.1 add.69
  54.3 0.1 add.70
  54.4 0.0 copy-done.1
  54.4 0.1 slice_reduce_fusion
  54.5 0.1 reshape_squeeze.3
  54.7 0.1 squeeze.8
  54.8 0.1 squeeze.9
  54.9 0.6 fusion.3.codes_ref
  55.5 20.3 %all-to-all-done.2 = f32[32,48,128]{2,1,0:T(8,128)S(1)} async-done(((f32[32,48,128]{2,1,0:T(8,128)}), f32[32,48,128]{2,1,0:T(8,128)S(1)}, u32[]{:S(2)}, u32[]{:S(2)}) %all-to-all-start.2) | async-done | bytes 786464 | tf_op jit(solution)/shard_map/all_to_all | solution.py:179
  75.7 0.0 copy-start
  75.7 0.9 copy-done
  76.6 56.0 %shard_map.66 = f32[32,3,8,128]{3,2,1,0:T(8,128)} custom-call(s32[512]{0:T(512)} %fusion.3.codes_ref, f32[1024,128]{1,0:T(8,128)} %bitcast.14, f32[32,6,8,128]{3,2,1,0:T(8,128)} %bitcast.12), custom_call_target="tpu_custom_call" | custom-call | tf_op jit(solution)/shard_map/pallas_call | solution.py:196
  132.6 23.9 %all_to_all.21 = f32[32,24,128]{2,1,0:T(8,128)} all-to-all(f32[32,24,128]{2,1,0:T(8,128)} %bitcast.16), channel_id=1, replica_groups=mesh['grp'=4,'zh'=4,'zl'=4,'y'=4,'core'=2] {'zl','y','core'}, dimensions={0} | all-to-all | bytes 786432 | tf_op jit(solution)/shard_map/all_to_all | solution.py:206
  156.5 2.0 %shard_map.67 = f32[3,128,128]{2,1,0:T(8,128)} custom-call(bf16[128,256]{1,0:T(8,128)(2,1)} %get-tuple-element.7.pick_ref, f32[32,3,8,128]{3,2,1,0:T(8,128)} %bitcast.15), custom_call_target="tpu_custom_call" | custom-call | tf_op jit(solution)/shard_map/pallas_call | solution.py:209
  (4 shorter events, 0.1 us)
Async XLA Ops:
  0.0 1.3 copy-start.2
  32.7 10.9 %all-to-all-start.1 = ((f32[4,256,128]{2,1,0:T(8,128)}), f32[4,256,128]{2,1,0:T(8,128)S(1)}, u32[]{:S(2)}, u32[]{:S(2)}) async-start(f32[4,256,128]{2,1,0:T(8,128)} %broadcast_in_dim.11), calls=%async_computation.1 | async-start | bytes 1048576 | tf_op jit(solution)/shard_map/all_to_all | solution.py:171
  43.6 10.8 %copy-start.1 = (f32[4,256,128]{2,1,0:T(8,128)}, f32[4,256,128]{2,1,0:T(8,128)S(1)}, u32[]{:S(2)}) copy-start(f32[4,256,128]{2,1,0:T(8,128)S(1)} %all-to-all-done.1) | copy-start | bytes 1572868
  43.6 32.1 %all-to-all-start.2 = ((f32[32,48,128]{2,1,0:T(8,128)}), f32[32,48,128]{2,1,0:T(8,128)S(1)}, u32[]{:S(2)}, u32[]{:S(2)}) async-start(f32[32,48,128]{2,1,0:T(8,128)} %bitcast.17), calls=%async_computation.2 | async-start | bytes 1572864 | tf_op jit(solution)/shard_map/all_to_all | solution.py:179
  75.7 0.9 copy-start

commit v2 on v1

v2 whole, which is shorter than its diff:
```python
import functools
import math

import jax
import jax.numpy as jnp
from jax import lax
from jax.experimental import pallas as pl
from jax.experimental.pallas import tpu as pltpu
from jax.sharding import Mesh
from jax.sharding import PartitionSpec as P


BLK = 128
COPIES = 4
TIME_STEP = 0.5
STIFFNESS = 0.5
RADIUS_SQ = 0.5
SCALE = math.sqrt(math.log2(math.e) / RADIUS_SQ)
GRP_DOM = ("grp", "zh", "zl", "y", "core")
NEAR = ("zl", "y", "core")
VMEM = pl.BlockSpec(memory_space=pltpu.VMEM)
SMEM = pl.BlockSpec(memory_space=pltpu.SMEM)
TOGETHER = 4
NOBODY = 256


def room(mib):
    return pltpu.CompilerParams(vmem_limit_bytes=mib << 20)


def lane_pick(row, index):
    return jnp.take_along_axis(row, index, axis=1, mode="promise_in_bounds")


def geometry_kernel(nodes_ref, conn_ref, seg_ref, slot_ref, out_ref):
    blocks = conn_ref.shape[1] // BLK
    parts = nodes_ref.shape[1] // BLK
    index = [
        jnp.concatenate([conn_ref[k : k + 1, b * BLK : (b + 1) * BLK] for b in range(blocks)], axis=0)
        for k in range(3)
    ]
    lanes = [i & (BLK - 1) for i in index]
    part = [i >> 7 for i in index]
    corner = [[None] * 6 for _ in range(3)]
    for comp in range(6):
        for p in range(parts):
            row = jnp.broadcast_to(nodes_ref[comp : comp + 1, p * BLK : (p + 1) * BLK], (blocks, BLK))
            for k in range(3):
                got = lane_pick(row, lanes[k])
                corner[k][comp] = got if p == 0 else jnp.where(part[k] == p, got, corner[k][comp])
    a, b, c = corner
    e = [b[i] - a[i] for i in range(3)]
    f = [c[i] - a[i] for i in range(3)]
    n = [
        0.5 * (e[1] * f[2] - e[2] * f[1]),
        0.5 * (e[2] * f[0] - e[0] * f[2]),
        0.5 * (e[0] * f[1] - e[1] * f[0]),
    ]
    m = [(a[i] + b[i] + c[i]) / 3.0 for i in range(3)]
    u = [(a[i] + b[i] + c[i]) / 3.0 for i in range(3, 6)]
    s = sum(n[i] * (m[i] + TIME_STEP * u[i]) for i in range(3))
    rows = [m[i] * (2.0 * SCALE) for i in range(3)] + [-v for v in n] + [s]
    groups, each = slot_ref.shape[1:]
    tables = jnp.concatenate([slot_ref[0], seg_ref[0]], axis=0).astype(jnp.float32)
    tables = jnp.concatenate([tables, jnp.zeros((2 * groups, BLK - each), jnp.float32)], axis=1)
    for i, row in enumerate(rows + [tables]):
        out_ref[:, i, :] = row


def three_parts(x):
    high = x.astype(jnp.bfloat16)
    rest = x - high.astype(jnp.float32)
    mid = rest.astype(jnp.bfloat16)
    low = (rest - mid.astype(jnp.float32)).astype(jnp.bfloat16)
    return high, mid, low


def exact_dot(onehot, x):
    return sum(jnp.dot(onehot, part, preferred_element_type=jnp.float32) for part in three_parts(x))


def place_kernel(copies, near, dest_ref, nodes_ref, out_ref, pick_ref):
    blocks = dest_ref.shape[1]
    slots = near * copies * 2
    across = jnp.broadcast_to(dest_ref[...].astype(jnp.float32), (blocks, blocks))
    down = across.T
    i = lax.broadcasted_iota(jnp.int32, (blocks, blocks), 0)
    j = lax.broadcasted_iota(jnp.int32, (blocks, blocks), 1)
    same = across == down

    def slot_of(dest, rank):
        dest = dest.astype(jnp.int32)
        return ((dest & (near - 1)) * copies + lax.div(dest, near)) * 2 + rank.astype(jnp.int32)

    rank_row = jnp.sum(jnp.where(same & (i < j), 1.0, 0.0), axis=0, keepdims=True)
    slot_row = slot_of(dest_ref[...], rank_row)
    onehot = (lax.broadcasted_iota(jnp.int32, (slots, blocks), 0) == slot_row).astype(jnp.float32).astype(jnp.bfloat16)
    rank_col = jnp.sum(jnp.where(same & (j < i), 1.0, 0.0), axis=1, keepdims=True)
    slot_col = slot_of(down[:, 0:1], rank_col)
    pick_ref[...] = (
        (lax.broadcasted_iota(jnp.int32, (blocks, slots), 1) == slot_col).astype(jnp.float32).astype(jnp.bfloat16)
    )
    for comp in range(6):
        x = nodes_ref[comp % 3]
        row = x * SCALE if comp < 3 else x + TIME_STEP * nodes_ref[comp]
        out_ref[:, comp] = exact_dot(onehot, row).reshape(near, copies * 2, BLK)


def start_kernel(copies, near, dest_ref, nodes_ref, corners_ref, conn_ref, seg_ref, slot_ref, out_ref, pick_ref, geo_ref):
    geometry_kernel(corners_ref, conn_ref, seg_ref, slot_ref, geo_ref)
    place_kernel(copies, near, dest_ref, nodes_ref, out_ref, pick_ref)


def split_two(x):
    high = x.astype(jnp.bfloat16).astype(jnp.float32)
    return high, x - high


def split_three(x):
    high, rest = split_two(x)
    mid, low = split_two(rest)
    return high, mid, low


def ready_kernel(codes_ref, geo_ref, todo_ref, count_ref, left_ref, normal_ref):
    steps = left_ref.shape[0]
    each = codes_ref.shape[0] // steps
    row = lax.broadcasted_iota(jnp.int32, (8, BLK), 0)
    ends = [jnp.full((8, BLK), -1.0, jnp.float32), jnp.zeros((8, BLK), jnp.float32)]

    def two_blocks(b, count):
        stack = []
        for half in range(2):
            tile = geo_ref[pl.ds(pl.multiple_of(b * 16 + half * 8, 8), 8), :]
            square = jnp.sum(jnp.where(row < 3, tile * tile, 0.0), axis=0, keepdims=True) * -0.25
            high, mid, low = split_three(jnp.where(row == 7, square, tile))
            stack += [high, high, high, mid, mid, low] + ends
            high, low = split_two(tile[3:6])
            normal = jnp.concatenate([high, low, jnp.zeros((2, BLK), jnp.float32)], axis=0)
            normal_ref[b * 2 + half] = normal.astype(jnp.bfloat16)
        left_ref[b] = jnp.concatenate(stack, axis=0).astype(jnp.bfloat16).T
        for k in range(each):
            code = codes_ref[b * each + k]
            todo_ref[count] = code
            count = count + jnp.where(code >= 0, 1, 0)
        return count

    count = lax.fori_loop(0, steps, two_blocks, jnp.int32(0))
    for k in range(2 * TOGETHER):
        todo_ref[count + k] = NOBODY
    count_ref[0] = count


def force_kernel(todo_ref, count_ref, left_ref, normal_ref, nodes_ref, out_ref, total, press):
    near, _, slots, _ = out_ref.shape
    total[...] = jnp.zeros_like(total)
    row = lax.broadcasted_iota(jnp.int32, (8, BLK), 0)
    is_close = (row >= 3) & (row < 7)
    is_far = (row < 3) | (row == 7)
    zero = jnp.zeros((8, BLK), jnp.float32)
    nothing = jnp.zeros((64, 2 * BLK), jnp.bfloat16)

    def begin(k):
        for n in range(TOGETHER):
            code = todo_ref[k * TOGETHER + n]
            slot = code & 511
            block = code >> 9
            source = jnp.minimum(lax.div(slot, slots), near - 1)
            start = source * (6 * slots) + lax.rem(slot, slots)
            tile = nodes_ref[pl.ds(start, 6, stride=slots), :]
            square = jnp.sum(tile[0:3] * tile[0:3], axis=0, keepdims=True)
            high, mid, low = split_three(
                jnp.concatenate([tile, jnp.ones((2, BLK), jnp.float32)], axis=0)
            )
            order = [high, mid, low, high, mid, high]
            close = [jnp.where(is_close, part, 0.0) for part in order] + [zero, zero]
            high, mid, low = split_three(square)
            last = jnp.where(row == 0, high, jnp.where(row == 1, mid, jnp.where(row == 2, low, 0.0)))
            far = [jnp.where(is_far, part, 0.0) for part in order] + [last, zero]
            right = jnp.concatenate(
                [
                    jnp.concatenate(close, axis=0).astype(jnp.bfloat16),
                    jnp.concatenate(far, axis=0).astype(jnp.bfloat16),
                ],
                axis=1,
            )
            first = (block & 1) == 0
            right = jnp.concatenate(
                [jnp.where(first, right, nothing), jnp.where(first, nothing, right)], axis=0
            )
            both = jnp.dot(left_ref[block >> 1], right, preferred_element_type=jnp.float32)
            pressure = jnp.exp2(both[:, BLK:]) * jnp.maximum(both[:, :BLK], 0.0)
            high = pressure.astype(jnp.bfloat16)
            press[n, 0:BLK] = high
            press[n, BLK:] = (pressure - high.astype(jnp.float32)).astype(jnp.bfloat16)

    def finish(k):
        for n in range(TOGETHER):
            code = todo_ref[k * TOGETHER + n]
            normal = normal_ref[code >> 9]
            normal = jnp.concatenate([normal, normal], axis=1)
            force = jnp.dot(normal, press[n], preferred_element_type=jnp.float32)
            at = pl.ds(pl.multiple_of((code & 511) * 8, 8), 8)
            total[at, :] = total[at, :] + (force + pltpu.roll(force, 5, 0))

    def step(k, _):
        finish(k)
        begin(k + 1)
        return 0

    steps = lax.div(count_ref[0] + (TOGETHER - 1), TOGETHER)
    begin(0)
    lax.fori_loop(0, steps, step, 0)
    for source in range(near):
        for comp in range(3):
            for half in range(slots // 8):
                out_ref[source, comp, half * 8 : half * 8 + 8, :] = total[
                    pl.ds((source * slots + half * 8) * 8 + comp, 8, stride=8), :
                ]


def pick_kernel(pick_ref, back_ref, out_ref):
    for comp in range(3):
        rows = back_ref[:, comp].reshape(pick_ref.shape[1], BLK)
        out_ref[comp] = -STIFFNESS * exact_dot(pick_ref[...], rows)


def f32(*shape):
    return jax.ShapeDtypeStruct(shape, jnp.float32)


def contact(node_state, node_dest, seg_nodes, seg_conn, pair_seg, pair_slot):
    groups = lax.axis_size("grp")
    copies = lax.axis_size("zh")
    near = lax.axis_size(NEAR)
    blocks = node_state.shape[0]
    seg_blocks = seg_conn.shape[1] // BLK
    per_group = pair_seg.shape[2]
    slots = copies * 2
    owners = groups * copies
    total_blocks = owners * seg_blocks

    outgoing, pick, geometry = pl.pallas_call(
        functools.partial(start_kernel, copies, near),
        out_shape=(
            f32(near, 6, slots, BLK),
            jax.ShapeDtypeStruct((blocks, near * slots), jnp.bfloat16),
            f32(seg_blocks, 8, BLK),
        ),
        in_specs=[VMEM] * 6,
        out_specs=[VMEM] * 3,
    )(
        node_dest.reshape(1, blocks),
        jnp.transpose(node_state, (1, 0, 2)),
        seg_nodes,
        seg_conn,
        pair_seg,
        pair_slot,
    )
    received = lax.all_to_all(
        outgoing.reshape(near, 6 * slots, BLK), NEAR, split_axis=0, concat_axis=0, tiled=True
    )
    geometry = lax.all_gather(geometry.reshape(seg_blocks * 8, BLK), "zh", axis=0, tiled=True)
    geometry = lax.all_gather(geometry, "grp", axis=0, tiled=True)

    tables = geometry.reshape(owners, seg_blocks, 8, BLK)[:, :, 7, :per_group].astype(jnp.int32)
    row = lax.axis_index("grp")
    slot = lax.dynamic_index_in_dim(tables, row, axis=1, keepdims=False)
    seg = lax.dynamic_index_in_dim(tables, row + groups, axis=1, keepdims=False)
    owner = jnp.arange(owners, dtype=jnp.int32)[:, None]
    source = slot // 2
    place = (owner % copies) * 2 + slot % 2
    block = owner * seg_blocks + seg
    codes = (source % near) * slots + place + block * 512
    codes = jnp.where(source // near == lax.axis_index("zh"), codes, -1).reshape(-1)

    todo, count, left, normal = pl.pallas_call(
        ready_kernel,
        out_shape=(
            jax.ShapeDtypeStruct((codes.shape[0] + 2 * TOGETHER,), jnp.int32),
            jax.ShapeDtypeStruct((1,), jnp.int32),
            jax.ShapeDtypeStruct((total_blocks // 2, BLK, BLK), jnp.bfloat16),
            jax.ShapeDtypeStruct((total_blocks, 8, BLK), jnp.bfloat16),
        ),
        in_specs=[SMEM, VMEM],
        out_specs=[SMEM, SMEM, VMEM, VMEM],
        compiler_params=room(14),
    )(codes, geometry.reshape(total_blocks * 8, BLK))
    forces = pl.pallas_call(
        force_kernel,
        out_shape=f32(near, 3, slots, BLK),
        in_specs=[SMEM, SMEM, VMEM, VMEM, VMEM],
        out_specs=VMEM,
        scratch_shapes=[
            pltpu.VMEM(((near * slots + 1) * 8, BLK), jnp.float32),
            pltpu.VMEM((TOGETHER, 2 * BLK, BLK), jnp.bfloat16),
        ],
        compiler_params=room(20),
    )(todo, count, left, normal, received.reshape(near * 6 * slots, BLK))
    back = lax.all_to_all(
        forces.reshape(near, 3 * slots, BLK), NEAR, split_axis=0, concat_axis=0, tiled=True
    )
    out = pl.pallas_call(
        pick_kernel,
        out_shape=f32(3, blocks, BLK),
        in_specs=[VMEM] * 2,
        out_specs=VMEM,
        compiler_params=room(4),
    )(pick, back.reshape(near, 3, slots, BLK))
    return jnp.transpose(out, (1, 0, 2))


def solution(mesh):
    groups = mesh.shape["grp"]
    split = Mesh(mesh.devices.reshape(groups, COPIES, 16 // COPIES, 4, 2), GRP_DOM)
    placed = (
        P(GRP_DOM, None, None),
        P(GRP_DOM),
        P(None, GRP_DOM),
        P(None, GRP_DOM),
        P(GRP_DOM, None, None),
        P(GRP_DOM, None, None),
    )
    return jax.shard_map(contact, mesh=split, in_specs=placed, out_specs=P(GRP_DOM, None, None), check_vma=False)
```

time: 160 us -> 105 us (0.66)
  Pallas kernels: 62.2 us -> 19.2 us
  waiting for transfers between devices: 24.7 us -> 0.01 us
  blocking collectives: 52.2 us -> 72.4 us
  starting transfers between devices: 14.5 us -> 10.4 us
  local copies, waits for them, and re-layouts: 4.29 us -> 2.16 us
    pallas_call x4, Pallas kernels: 62.2 us -> 19.2 us  [the longest x1 9.18 us: contact(): pl.pallas_call(force_kernel, out_shape=f32(near, 3, slots, BLK), in_specs...]
    all_gather x0 -> x2, blocking collectives: none -> 39.6 us  [the longest x1 29.2 us: contact(): lax.all_gather(geometry.reshape(seg_blocks * 8, BLK), 'zh', axis=0, tiled...]
    all_to_all x2 -> x1, waiting for transfers between devices: 24.7 us -> 0.01 us  [contact(): lax.all_to_all(outgoing.reshape(near, 6 * slots, BLK), NEAR, split_axis=0...]
    all_to_all x2 -> x1, blocking collectives: 52.2 us -> 32.8 us  [contact(): lax.all_to_all(forces.reshape(near, 3 * slots, BLK), NEAR, split_axis=0,...]
    all_to_all x2 -> x1, starting transfers between devices: 14.5 us -> 10.4 us  [contact(): lax.all_to_all(outgoing.reshape(near, 6 * slots, BLK), NEAR, split_axis=0...]
    reshape x2 -> x0, local copies, waits for them, and re-layouts: 1.9 us -> none  [the longest x1 1.28 us: shards(): pair_seg.reshape(1, BLK)]
  transfers between devices with their start and end apart: 2 -> 1, of which waited for: 2 -> 0; matrix products, arithmetic and copies ran while one was open for 1% -> 1% of each run, Pallas kernels for 2% -> 6%
where the time goes in v2:
time: 105 us; the launch traced here: 104 us
  blocking collectives  72.4 us (69%)
  Pallas kernels  19.2 us (18%)
  starting transfers between devices  10.4 us (10%)
  local copies, waits for them, and re-layouts  2.16 us (2%)
    all_to_all x1, blocking collectives, contact(): lax.all_to_all(forces.reshape(near, 3 * slots, BLK), NEAR, split_axis=0,...  32.8 us
    all_gather x1, blocking collectives, contact(): lax.all_gather(geometry.reshape(seg_blocks * 8, BLK), 'zh', axis=0, tiled...  29.2 us
    all_to_all x1, starting transfers between devices, contact(): lax.all_to_all(outgoing.reshape(near, 6 * slots, BLK), NEAR, split_axis=0...  10.4 us
    all_gather x1, blocking collectives, contact(): geometry = lax.all_gather(geometry, 'grp', axis=0, tiled=True)  10.4 us
    pallas_call x1, Pallas kernels, contact(): pl.pallas_call(force_kernel, out_shape=f32(near, 3, slots, BLK), in_specs...  9.18 us
    pallas_call x1, Pallas kernels, contact(): pl.pallas_call(ready_kernel, out_shape=(jax.ShapeDtypeStruct((codes.shape...  6.53 us
    pallas_call x1, Pallas kernels, contact(): pl.pallas_call(functools.partial(start_kernel, copies, near), out_shape=(...  2.47 us
  transfers between devices with their start and end apart: 1, of which 0 were waited for; matrix products, arithmetic and copies ran while one was open for 1% of the time, Pallas kernels for 6%

profile of v2, /device:TPU:1, one launch (start us, length us, event | category | flops | bytes accessed | tf_op | source)
XLA Modules:
  0.0 104.3 jit_solution(5431446855763269471)
XLA Ops:
  0.0 2.5 %shard_map.64 = (f32[32,6,8,128]{3,2,1,0:T(8,128)}, bf16[128,256]{1,0:T(8,128)(2,1)}, f32[8,8,128]{2,1,0:T(8,128)}) custom-call(s32[1,128]{1,0:T(1,128)} %bitcast.16, f32[6,128,128]{2,1,0:T(8,128)} %bitcast.14, f32[6,512]{1,0:T(8,128)} %corners_ref.1, s32[3,1024]{1,0:T(4,128)} %conn_ref.1, s32[1,4,32]{2,1,0:T(4,128)} %seg_ref.1, s32[1,4,32]{2,1,0:T(4,128)} %slot_ref.1), custom_call_target="tpu_custom_call" | custom-call | tf_op jit(solution)/shard_map/pallas_call | solution.py:243
  2.5 10.4 %all-to-all-start = ((f32[32,48,128]{2,1,0:T(8,128)}), f32[32,48,128]{2,1,0:T(8,128)S(1)}, u32[]{:S(2)}, u32[]{:S(2)}) async-start(f32[32,48,128]{2,1,0:T(8,128)} %bitcast.13), calls=%async_computation | async-start | bytes 1572864 | tf_op jit(solution)/shard_map/all_to_all | solution.py:260
  12.9 0.1 add.72
  13.0 0.1 add.73
  13.1 0.1 add.77
  13.1 0.1 add.78
  13.2 29.2 %all_gather.6 = f32[256,128]{1,0:T(8,128)S(1)} all-gather(f32[64,128]{1,0:T(8,128)} %bitcast.15), channel_id=1, replica_groups=mesh['grp'=4,'zh'=4,'zl'=4,'y'=4,'core'=2] {'zh'}, dimensions={0}, use_global_device_ids=true | all-gather | bytes 163840 | tf_op jit(solution)/shard_map/all_gather | solution.py:263
  42.4 10.4 %all_gather.7.geo_ref = f32[1024,128]{1,0:T(8,128)S(1)} all-gather(f32[256,128]{1,0:T(8,128)S(1)} %all_gather.6), channel_id=1, replica_groups=mesh['grp'=4,'zh'=4,'zl'=4,'y'=4,'core'=2] {'grp'}, dimensions={0}, use_global_device_ids=true | all-gather | bytes 655360 | tf_op jit(solution)/shard_map/all_gather | solution.py:264
  52.8 0.1 slice_convert_fusion
  52.8 0.1 dynamic-slice_reduce_fusion.1
  52.9 0.1 squeeze.8
  53.0 0.1 squeeze.9
  53.1 6.5 %shard_map.65 = (s32[520]{0:T(1024)S(1)}, s32[1]{0:T(128)}, bf16[64,128,128]{2,1,0:T(8,128)(2,1)S(1)}, bf16[128,8,128]{2,1,0:T(8,128)(2,1)S(1)}) custom-call(s32[512]{0:T(512)S(1)} %fusion.4.codes_ref, f32[1024,128]{1,0:T(8,128)S(1)} %all_gather.7.geo_ref), custom_call_target="tpu_custom_call" | custom-call | tf_op jit(solution)/shard_map/pallas_call | solution.py:277
  59.6 0.0 copy-start
  59.6 0.7 copy-done
  60.3 0.0 all-to-all-done
  60.3 0.0 copy-start.1
  60.3 0.9 copy-done.1
  61.3 0.0 copy-start.2
  61.3 9.2 %shard_map.66 = f32[32,3,8,128]{3,2,1,0:T(8,128)S(1)} custom-call(s32[520]{0:T(1024)S(1)} %get-tuple-element.14.todo_ref, s32[1]{0:T(128)} %get-tuple-element.15.count_ref, bf16[64,128,128]{2,1,0:T(8,128)(2,1)S(1)} %get-tuple-element.16.left_ref, bf16[128,8,128]{2,1,0:T(8,128)(2,1)S(1)} %copy-done.1, f32[1536,128]{1,0:T(8,128)S(1)} %bitcast.9), custom_call_target="tpu_custom_call" | custom-call | tf_op jit(solution)/shard_map/pallas_call | solution.py:289
  70.5 32.8 %all_to_all.10 = f32[32,24,128]{2,1,0:T(8,128)S(1)} all-to-all(f32[32,24,128]{2,1,0:T(8,128)S(1)} %bitcast.11), channel_id=1, replica_groups=mesh['grp'=4,'zh'=4,'zl'=4,'y'=4,'core'=2] {'zl','y','core'}, dimensions={0} | all-to-all | bytes 786432 | tf_op jit(solution)/shard_map/all_to_all | solution.py:300
  103.3 0.0 copy-done.2
  103.3 1.0 shard_map.67
  (3 shorter events, 0.0 us)
Async XLA Ops:
  2.5 57.8 %all-to-all-start = ((f32[32,48,128]{2,1,0:T(8,128)}), f32[32,48,128]{2,1,0:T(8,128)S(1)}, u32[]{:S(2)}, u32[]{:S(2)}) async-start(f32[32,48,128]{2,1,0:T(8,128)} %bitcast.13), calls=%async_computation | async-start | bytes 1572864 | tf_op jit(solution)/shard_map/all_to_all | solution.py:260
  59.6 0.7 copy-start
  60.3 1.0 copy-start.1
  61.3 42.0 %copy-start.2 = (bf16[128,256]{1,0:T(8,128)(2,1)S(1)}, bf16[128,256]{1,0:T(8,128)(2,1)}, u32[]{:S(2)}) copy-start(bf16[128,256]{1,0:T(8,128)(2,1)} %get-tuple-element.12.pick_ref) | copy-start | bytes 196612

commit v3 on v2

--- a/solution.py
+++ b/solution.py
@@ -20,7 +20,7 @@
 NEAR = ("zl", "y", "core")
 VMEM = pl.BlockSpec(memory_space=pltpu.VMEM)
 SMEM = pl.BlockSpec(memory_space=pltpu.SMEM)
-TOGETHER = 4
+TOGETHER = 8
 NOBODY = 256
 
 
@@ -63,8 +63,9 @@
     groups, each = slot_ref.shape[1:]
     tables = jnp.concatenate([slot_ref[0], seg_ref[0]], axis=0).astype(jnp.float32)
     tables = jnp.concatenate([tables, jnp.zeros((2 * groups, BLK - each), jnp.float32)], axis=1)
-    for i, row in enumerate(rows + [tables]):
-        out_ref[:, i, :] = row
+    for copy in range(out_ref.shape[0]):
+        for i, row in enumerate(rows + [tables]):
+            out_ref[copy, :, i, :] = row
 
 
 def three_parts(x):
@@ -106,11 +107,6 @@
         out_ref[:, comp] = exact_dot(onehot, row).reshape(near, copies * 2, BLK)
 
 
-def start_kernel(copies, near, dest_ref, nodes_ref, corners_ref, conn_ref, seg_ref, slot_ref, out_ref, pick_ref, geo_ref):
-    geometry_kernel(corners_ref, conn_ref, seg_ref, slot_ref, geo_ref)
-    place_kernel(copies, near, dest_ref, nodes_ref, out_ref, pick_ref)
-
-
 def split_two(x):
     high = x.astype(jnp.bfloat16).astype(jnp.float32)
     return high, x - high
@@ -122,7 +118,7 @@
     return high, mid, low
 
 
-def ready_kernel(codes_ref, geo_ref, todo_ref, count_ref, left_ref, normal_ref):
+def ready_kernel(codes_ref, geo_ref, todo_ref, count_ref, left_ref):
     steps = left_ref.shape[0]
     each = codes_ref.shape[0] // steps
     row = lax.broadcasted_iota(jnp.int32, (8, BLK), 0)
@@ -135,9 +131,6 @@
             square = jnp.sum(jnp.where(row < 3, tile * tile, 0.0), axis=0, keepdims=True) * -0.25
             high, mid, low = split_three(jnp.where(row == 7, square, tile))
             stack += [high, high, high, mid, mid, low] + ends
-            high, low = split_two(tile[3:6])
-            normal = jnp.concatenate([high, low, jnp.zeros((2, BLK), jnp.float32)], axis=0)
-            normal_ref[b * 2 + half] = normal.astype(jnp.bfloat16)
         left_ref[b] = jnp.concatenate(stack, axis=0).astype(jnp.bfloat16).T
         for k in range(each):
             code = codes_ref[b * each + k]
@@ -145,13 +138,13 @@
             count = count + jnp.where(code >= 0, 1, 0)
         return count
 
-    count = lax.fori_loop(0, steps, two_blocks, jnp.int32(0))
+    count = lax.fori_loop(0, steps, two_blocks, jnp.int32(0), unroll=4)
     for k in range(2 * TOGETHER):
         todo_ref[count + k] = NOBODY
     count_ref[0] = count
 
 
-def force_kernel(todo_ref, count_ref, left_ref, normal_ref, nodes_ref, out_ref, total, press):
+def force_kernel(todo_ref, count_ref, left_ref, geo_ref, nodes_ref, out_ref, total, press):
     near, _, slots, _ = out_ref.shape
     total[...] = jnp.zeros_like(total)
     row = lax.broadcasted_iota(jnp.int32, (8, BLK), 0)
@@ -197,11 +190,12 @@
     def finish(k):
         for n in range(TOGETHER):
             code = todo_ref[k * TOGETHER + n]
-            normal = normal_ref[code >> 9]
+            tile = geo_ref[pl.ds(pl.multiple_of((code >> 9) * 8, 8), 8), :]
+            normal = jnp.concatenate(split_two(tile), axis=0).astype(jnp.bfloat16)
             normal = jnp.concatenate([normal, normal], axis=1)
             force = jnp.dot(normal, press[n], preferred_element_type=jnp.float32)
             at = pl.ds(pl.multiple_of((code & 511) * 8, 8), 8)
-            total[at, :] = total[at, :] + (force + pltpu.roll(force, 5, 0))
+            total[at, :] = total[at, :] + (force[0:8] + force[8:16])
 
     def step(k, _):
         finish(k)
@@ -215,7 +209,7 @@
         for comp in range(3):
             for half in range(slots // 8):
                 out_ref[source, comp, half * 8 : half * 8 + 8, :] = total[
-                    pl.ds((source * slots + half * 8) * 8 + comp, 8, stride=8), :
+                    pl.ds((source * slots + half * 8) * 8 + 3 + comp, 8, stride=8), :
                 ]
 
 
@@ -240,27 +234,29 @@
     owners = groups * copies
     total_blocks = owners * seg_blocks
 
-    outgoing, pick, geometry = pl.pallas_call(
-        functools.partial(start_kernel, copies, near),
-        out_shape=(
-            f32(near, 6, slots, BLK),
-            jax.ShapeDtypeStruct((blocks, near * slots), jnp.bfloat16),
-            f32(seg_blocks, 8, BLK),
-        ),
-        in_specs=[VMEM] * 6,
-        out_specs=[VMEM] * 3,
-    )(
-        node_dest.reshape(1, blocks),
-        jnp.transpose(node_state, (1, 0, 2)),
-        seg_nodes,
-        seg_conn,
-        pair_seg,
-        pair_slot,
-    )
+    geometry = pl.pallas_call(
+        geometry_kernel,
+        out_shape=f32(1, seg_blocks, 8, BLK),
+        in_specs=[VMEM] * 4,
+        out_specs=VMEM,
+    )(seg_nodes, seg_conn, pair_seg, pair_slot)
+    outgoing, pick = pl.pallas_call(
+        functools.partial(place_kernel, copies, near),
+        out_shape=(f32(near, 6, slots, BLK), jax.ShapeDtypeStruct((blocks, near * slots), jnp.bfloat16)),
+        in_specs=[VMEM] * 2,
+        out_specs=[VMEM] * 2,
+    )(node_dest.reshape(1, blocks), jnp.transpose(node_state, (1, 0, 2)))
     received = lax.all_to_all(
         outgoing.reshape(near, 6 * slots, BLK), NEAR, split_axis=0, concat_axis=0, tiled=True
     )
-    geometry = lax.all_gather(geometry.reshape(seg_blocks * 8, BLK), "zh", axis=0, tiled=True)
+    geometry = geometry.reshape(seg_blocks * 8, BLK)
+    offset = jnp.zeros((1,), jnp.int32)
+    shift = 1
+    while shift < copies:
+        moved = lax.ppermute(geometry, "zh", [(i, i ^ shift) for i in range(copies)])
+        geometry = jnp.concatenate([geometry, moved], axis=0)
+        offset = jnp.concatenate([offset, offset ^ shift])
+        shift *= 2
     geometry = lax.all_gather(geometry, "grp", axis=0, tiled=True)
 
     tables = geometry.reshape(owners, seg_blocks, 8, BLK)[:, :, 7, :per_group].astype(jnp.int32)
@@ -269,23 +265,22 @@
     seg = lax.dynamic_index_in_dim(tables, row + groups, axis=1, keepdims=False)
     owner = jnp.arange(owners, dtype=jnp.int32)[:, None]
     source = slot // 2
-    place = (owner % copies) * 2 + slot % 2
+    place = (lax.axis_index("zh") ^ jnp.tile(offset, groups)[:, None]) * 2 + slot % 2
     block = owner * seg_blocks + seg
     codes = (source % near) * slots + place + block * 512
     codes = jnp.where(source // near == lax.axis_index("zh"), codes, -1).reshape(-1)
 
-    todo, count, left, normal = pl.pallas_call(
+    todo, count, left = pl.pallas_call(
         ready_kernel,
         out_shape=(
             jax.ShapeDtypeStruct((codes.shape[0] + 2 * TOGETHER,), jnp.int32),
             jax.ShapeDtypeStruct((1,), jnp.int32),
             jax.ShapeDtypeStruct((total_blocks // 2, BLK, BLK), jnp.bfloat16),
-            jax.ShapeDtypeStruct((total_blocks, 8, BLK), jnp.bfloat16),
         ),
         in_specs=[SMEM, VMEM],
-        out_specs=[SMEM, SMEM, VMEM, VMEM],
+        out_specs=[SMEM, SMEM, VMEM],
         compiler_params=room(14),
-    )(codes, geometry.reshape(total_blocks * 8, BLK))
+    )(codes, geometry)
     forces = pl.pallas_call(
         force_kernel,
         out_shape=f32(near, 3, slots, BLK),
@@ -296,7 +291,7 @@
             pltpu.VMEM((TOGETHER, 2 * BLK, BLK), jnp.bfloat16),
         ],
         compiler_params=room(20),
-    )(todo, count, left, normal, received.reshape(near * 6 * slots, BLK))
+    )(todo, count, left, geometry, received.reshape(near * 6 * slots, BLK))
     back = lax.all_to_all(
         forces.reshape(near, 3 * slots, BLK), NEAR, split_axis=0, concat_axis=0, tiled=True
     )

time: 105 us -> 104 us (level)
  blocking collectives: 72.4 us -> 49 us
  starting transfers between devices: 10.4 us -> 31.6 us
  waiting for transfers between devices: 0.01 us -> 4.77 us
  Pallas kernels: 19.2 us -> 15.2 us
  local copies, waits for them, and re-layouts: 2.16 us -> 0.6 us
  other arithmetic: 0.1 us -> 1.63 us
    all_gather x1 -> x0, blocking collectives: 29.2 us -> none  [contact(): lax.all_gather(geometry.reshape(seg_blocks * 8, BLK), 'zh', axis=0, tiled...]
    ppermute x0 -> x2, starting transfers between devices: none -> 21.2 us  [contact(): lax.ppermute(geometry, 'zh', [(i, i ^ shift) for i in range(copies)])]
    all_to_all x1, blocking collectives: 32.8 us -> 38.8 us  [contact(): lax.all_to_all(forces.reshape(near, 3 * slots, BLK), NEAR, split_axis=0,...]
    ppermute x0 -> x2, waiting for transfers between devices: none -> 4.77 us  [contact(): lax.ppermute(geometry, 'zh', [(i, i ^ shift) for i in range(copies)])]
    pallas_call x1, Pallas kernels: 6.53 us -> 3.04 us  [contact(): pl.pallas_call(ready_kernel, out_shape=(jax.ShapeDtypeStruct((codes.shape...]
    pallas_call x1, Pallas kernels: 9.18 us -> 7.1 us  [contact(): pl.pallas_call(force_kernel, out_shape=f32(near, 3, slots, BLK), in_specs...]
    unnamed x6 -> x2, local copies, waits for them, and re-layouts: 1.65 us -> 0.01 us
    pallas_call x1 -> x2, Pallas kernels: 2.47 us -> 4.09 us  [the longest x1 2.48 us: contact(): pl.pallas_call(functools.partial(place_kernel, copies, near), out_shape=(...]
  transfers between devices with their start and end apart: 1 -> 3, of which waited for: 0 -> 2; matrix products, arithmetic and copies ran while one was open for 1% -> 2% of each run, Pallas kernels for 6% -> 5%
where the time goes in v3:
time: 104 us; the launch traced here: 103 us
  blocking collectives  49 us (47%)
  starting transfers between devices  31.6 us (30%)
  Pallas kernels  15.2 us (15%)
  waiting for transfers between devices  4.77 us (5%)
  other arithmetic  1.63 us (2%)
    all_to_all x1, blocking collectives, contact(): lax.all_to_all(forces.reshape(near, 3 * slots, BLK), NEAR, split_axis=0,...  38.8 us
    ppermute x2, starting transfers between devices, contact(): lax.ppermute(geometry, 'zh', [(i, i ^ shift) for i in range(copies)])  21.2 us
    all_to_all x1, starting transfers between devices, contact(): lax.all_to_all(outgoing.reshape(near, 6 * slots, BLK), NEAR, split_axis=0...  10.4 us
    all_gather x1, blocking collectives, contact(): geometry = lax.all_gather(geometry, 'grp', axis=0, tiled=True)  10.2 us
    pallas_call x1, Pallas kernels, contact(): pl.pallas_call(force_kernel, out_shape=f32(near, 3, slots, BLK), in_specs...  7.1 us
    ppermute x2, waiting for transfers between devices, contact(): lax.ppermute(geometry, 'zh', [(i, i ^ shift) for i in range(copies)])  4.77 us
    pallas_call x1, Pallas kernels, contact(): pl.pallas_call(ready_kernel, out_shape=(jax.ShapeDtypeStruct((codes.shape...  3.04 us
    pallas_call x1, Pallas kernels, contact(): pl.pallas_call(functools.partial(place_kernel, copies, near), out_shape=(...  2.48 us
  transfers between devices with their start and end apart: 3, of which 2 were waited for; matrix products, arithmetic and copies ran while one was open for 2% of the time, Pallas kernels for 5%

profile of v3, /device:TPU:1, one launch (start us, length us, event | category | flops | bytes accessed | tf_op | source)
XLA Modules:
  0.0 103.0 jit_solution(10645149274104162436)
XLA Ops:
  0.0 2.5 %shard_map.64 = (f32[32,6,8,128]{3,2,1,0:T(8,128)}, bf16[128,256]{1,0:T(8,128)(2,1)}) custom-call(s32[1,128]{1,0:T(1,128)} %bitcast.18, f32[6,128,128]{2,1,0:T(8,128)} %bitcast.14), custom_call_target="tpu_custom_call" | custom-call | tf_op jit(solution)/shard_map/pallas_call | solution.py:243
  2.5 10.4 %all-to-all-start = ((f32[32,48,128]{2,1,0:T(8,128)}), f32[32,48,128]{2,1,0:T(8,128)S(1)}, u32[]{:S(2)}, u32[]{:S(2)}) async-start(f32[32,48,128]{2,1,0:T(8,128)} %bitcast.13), calls=%async_computation | async-start | bytes 1572864 | tf_op jit(solution)/shard_map/all_to_all | solution.py:249
  12.9 1.6 %shard_map.65 = f32[1,8,8,128]{3,2,1,0:T(8,128)} custom-call(f32[6,512]{1,0:T(8,128)} %nodes_ref.1, s32[3,1024]{1,0:T(4,128)} %conn_ref.1, s32[1,4,32]{2,1,0:T(4,128)} %seg_ref.1, s32[1,4,32]{2,1,0:T(4,128)} %slot_ref.1), custom_call_target="tpu_custom_call" | custom-call | tf_op jit(solution)/shard_map/pallas_call | solution.py:237
  14.5 8.6 %collective-permute-start = (f32[64,128]{1,0:T(8,128)}, f32[64,128]{1,0:T(8,128)S(1)}, u32[]{:S(2)}, u32[]{:S(2)}) collective-permute-start(f32[64,128]{1,0:T(8,128)} %bitcast.15), channel_id=1, source_target_pairs={{0,32},{32,0},{64,96},{96,64},{1,33},{33,1},{65,97},{97,65},{2,34}... | collective-permute-start | bytes 98312 | tf_op jit(solution)/shard_map/ppermute | solution.py:256
  23.1 0.1 mul.36
  23.2 0.1 add.60
  23.3 0.1 add.61
  23.4 3.2 %collective-permute-done = f32[64,128]{1,0:T(8,128)S(1)} collective-permute-done((f32[64,128]{1,0:T(8,128)}, f32[64,128]{1,0:T(8,128)S(1)}, u32[]{:S(2)}, u32[]{:S(2)}) %collective-permute-start) | collective-permute-done | bytes 32800 | tf_op jit(solution)/shard_map/ppermute | solution.py:256
  26.5 0.8 pad_maximum_fusion.1
  27.3 12.7 %collective-permute-start.1 = (f32[128,128]{1,0:T(8,128)S(1)}, f32[128,128]{1,0:T(8,128)S(1)}, u32[]{:S(2)}, u32[]{:S(2)}) collective-permute-start(f32[128,128]{1,0:T(8,128)S(1)} %pad_maximum_fusion.1), channel_id=1, source_target_pairs={{0,64},{32,96},{64,0},{96,32},{1,65},{33,97},{65,1},{97,33},{2,66}... | collective-permute-start | bytes 196616 | tf_op jit(solution)/shard_map/ppermute | solution.py:256
  40.0 0.1 add.65
  40.1 0.1 add.66
  40.1 1.6 %collective-permute-done.1 = f32[128,128]{1,0:T(8,128)S(1)} collective-permute-done((f32[128,128]{1,0:T(8,128)S(1)}, f32[128,128]{1,0:T(8,128)S(1)}, u32[]{:S(2)}, u32[]{:S(2)}) %collective-permute-start.1) | collective-permute-done | bytes 65568 | tf_op jit(solution)/shard_map/ppermute | solution.py:256
  41.7 0.8 pad_maximum_fusion
  42.5 10.2 %all_gather.3.geo_ref = f32[1024,128]{1,0:T(8,128)S(1)} all-gather(f32[256,128]{1,0:T(8,128)S(1)} %pad_maximum_fusion), channel_id=1, replica_groups=mesh['grp'=4,'zh'=4,'zl'=4,'y'=4,'core'=2] {'grp'}, dimensions={0}, use_global_device_ids=true | all-gather | bytes 655360 | tf_op jit(solution)/shard_map/all_gather | solution.py:260
  52.7 0.1 slice_convert_fusion
  52.8 0.1 dynamic-slice_reduce_fusion.1
  52.9 0.1 squeeze.8
  52.9 0.1 squeeze.9
  53.0 3.0 %shard_map.66 = (s32[528]{0:T(1024)S(1)}, s32[1]{0:T(128)}, bf16[64,128,128]{2,1,0:T(8,128)(2,1)S(1)}) custom-call(s32[512]{0:T(512)S(1)} %fusion.4.codes_ref, f32[1024,128]{1,0:T(8,128)S(1)} %all_gather.3.geo_ref), custom_call_target="tpu_custom_call" | custom-call | tf_op jit(solution)/shard_map/pallas_call | solution.py:273
  56.1 0.0 all-to-all-done
  56.1 0.0 copy-start
  56.1 7.1 %shard_map.67 = f32[32,3,8,128]{3,2,1,0:T(8,128)S(1)} custom-call(s32[528]{0:T(1024)S(1)} %get-tuple-element.11.todo_ref, s32[1]{0:T(128)} %get-tuple-element.12.count_ref, bf16[64,128,128]{2,1,0:T(8,128)(2,1)S(1)} %get-tuple-element.13.left_ref, f32[1024,128]{1,0:T(8,128)S(1)} %all_gather.3.geo_ref, f32[1536,128]{1,0:T(8,128)S(1)} %bitcast.10), custom_call_target="tpu_custom_call" | custom-call | tf_op jit(solution)/shard_map/pallas_call | solution.py:284
  63.2 38.8 %all_to_all.10 = f32[32,24,128]{2,1,0:T(8,128)S(1)} all-to-all(f32[32,24,128]{2,1,0:T(8,128)S(1)} %bitcast.11), channel_id=1, replica_groups=mesh['grp'=4,'zh'=4,'zl'=4,'y'=4,'core'=2] {'zl','y','core'}, dimensions={0} | all-to-all | bytes 786432 | tf_op jit(solution)/shard_map/all_to_all | solution.py:295
  102.0 0.0 copy-done
  102.0 1.0 shard_map.68
  (3 shorter events, 0.0 us)
Async XLA Ops:
  2.5 53.6 %all-to-all-start = ((f32[32,48,128]{2,1,0:T(8,128)}), f32[32,48,128]{2,1,0:T(8,128)S(1)}, u32[]{:S(2)}, u32[]{:S(2)}) async-start(f32[32,48,128]{2,1,0:T(8,128)} %bitcast.13), calls=%async_computation | async-start | bytes 1572864 | tf_op jit(solution)/shard_map/all_to_all | solution.py:249
  14.5 12.0 %collective-permute-start = (f32[64,128]{1,0:T(8,128)}, f32[64,128]{1,0:T(8,128)S(1)}, u32[]{:S(2)}, u32[]{:S(2)}) collective-permute-start(f32[64,128]{1,0:T(8,128)} %bitcast.15), channel_id=1, source_target_pairs={{0,32},{32,0},{64,96},{96,64},{1,33},{33,1},{65,97},{97,65},{2,34}... | collective-permute-start | bytes 98312 | tf_op jit(solution)/shard_map/ppermute | solution.py:256
  27.3 14.4 %collective-permute-start.1 = (f32[128,128]{1,0:T(8,128)S(1)}, f32[128,128]{1,0:T(8,128)S(1)}, u32[]{:S(2)}, u32[]{:S(2)}) collective-permute-start(f32[128,128]{1,0:T(8,128)S(1)} %pad_maximum_fusion.1), channel_id=1, source_target_pairs={{0,64},{32,96},{64,0},{96,32},{1,65},{33,97},{65,1},{97,33},{2,66}... | collective-permute-start | bytes 196616 | tf_op jit(solution)/shard_map/ppermute | solution.py:256
  56.1 45.9 %copy-start = (bf16[128,256]{1,0:T(8,128)(2,1)S(1)}, bf16[128,256]{1,0:T(8,128)(2,1)}, u32[]{:S(2)}) copy-start(bf16[128,256]{1,0:T(8,128)(2,1)} %get-tuple-element.10.pick_ref) | copy-start | bytes 196612

commit v4 on v2

--- a/solution.py
+++ b/solution.py
@@ -20,7 +20,7 @@
 NEAR = ("zl", "y", "core")
 VMEM = pl.BlockSpec(memory_space=pltpu.VMEM)
 SMEM = pl.BlockSpec(memory_space=pltpu.SMEM)
-TOGETHER = 4
+TOGETHER = 12
 NOBODY = 256
 
 
@@ -32,7 +32,7 @@
     return jnp.take_along_axis(row, index, axis=1, mode="promise_in_bounds")
 
 
-def geometry_kernel(nodes_ref, conn_ref, seg_ref, slot_ref, out_ref):
+def geometry_rows(nodes_ref, conn_ref, seg_ref, slot_ref, out_ref):
     blocks = conn_ref.shape[1] // BLK
     parts = nodes_ref.shape[1] // BLK
     index = [
@@ -79,7 +79,10 @@
     return sum(jnp.dot(onehot, part, preferred_element_type=jnp.float32) for part in three_parts(x))
 
 
-def place_kernel(copies, near, dest_ref, nodes_ref, out_ref, pick_ref):
+def start_kernel(
+    copies, near, dest_ref, nodes_ref, corners_ref, conn_ref, seg_ref, slot_ref, out_ref, pick_ref, geo_ref
+):
+    geometry_rows(corners_ref, conn_ref, seg_ref, slot_ref, geo_ref)
     blocks = dest_ref.shape[1]
     slots = near * copies * 2
     across = jnp.broadcast_to(dest_ref[...].astype(jnp.float32), (blocks, blocks))
@@ -106,11 +109,6 @@
         out_ref[:, comp] = exact_dot(onehot, row).reshape(near, copies * 2, BLK)
 
 
-def start_kernel(copies, near, dest_ref, nodes_ref, corners_ref, conn_ref, seg_ref, slot_ref, out_ref, pick_ref, geo_ref):
-    geometry_kernel(corners_ref, conn_ref, seg_ref, slot_ref, geo_ref)
-    place_kernel(copies, near, dest_ref, nodes_ref, out_ref, pick_ref)
-
-
 def split_two(x):
     high = x.astype(jnp.bfloat16).astype(jnp.float32)
     return high, x - high
@@ -122,49 +120,28 @@
     return high, mid, low
 
 
-def ready_kernel(codes_ref, geo_ref, todo_ref, count_ref, left_ref, normal_ref):
-    steps = left_ref.shape[0]
-    each = codes_ref.shape[0] // steps
-    row = lax.broadcasted_iota(jnp.int32, (8, BLK), 0)
-    ends = [jnp.full((8, BLK), -1.0, jnp.float32), jnp.zeros((8, BLK), jnp.float32)]
-
-    def two_blocks(b, count):
-        stack = []
-        for half in range(2):
-            tile = geo_ref[pl.ds(pl.multiple_of(b * 16 + half * 8, 8), 8), :]
-            square = jnp.sum(jnp.where(row < 3, tile * tile, 0.0), axis=0, keepdims=True) * -0.25
-            high, mid, low = split_three(jnp.where(row == 7, square, tile))
-            stack += [high, high, high, mid, mid, low] + ends
-            high, low = split_two(tile[3:6])
-            normal = jnp.concatenate([high, low, jnp.zeros((2, BLK), jnp.float32)], axis=0)
-            normal_ref[b * 2 + half] = normal.astype(jnp.bfloat16)
-        left_ref[b] = jnp.concatenate(stack, axis=0).astype(jnp.bfloat16).T
-        for k in range(each):
-            code = codes_ref[b * each + k]
-            todo_ref[count] = code
-            count = count + jnp.where(code >= 0, 1, 0)
-        return count
-
-    count = lax.fori_loop(0, steps, two_blocks, jnp.int32(0))
-    for k in range(2 * TOGETHER):
-        todo_ref[count + k] = NOBODY
-    count_ref[0] = count
-
-
-def force_kernel(todo_ref, count_ref, left_ref, normal_ref, nodes_ref, out_ref, total, press):
+def force_kernel(codes_ref, geo_ref, nodes_ref, out_ref, total, press, todo_ref):
     near, _, slots, _ = out_ref.shape
     total[...] = jnp.zeros_like(total)
     row = lax.broadcasted_iota(jnp.int32, (8, BLK), 0)
     is_close = (row >= 3) & (row < 7)
     is_far = (row < 3) | (row == 7)
     zero = jnp.zeros((8, BLK), jnp.float32)
-    nothing = jnp.zeros((64, 2 * BLK), jnp.bfloat16)
+    minus = jnp.full((8, BLK), -1.0, jnp.float32)
+
+    def geometry(code):
+        return geo_ref[pl.ds(pl.multiple_of((code >> 9) * 8, 8), 8), :]
 
     def begin(k):
         for n in range(TOGETHER):
             code = todo_ref[k * TOGETHER + n]
+            tile = geometry(code)
+            square = jnp.sum(jnp.where(row < 3, tile * tile, 0.0), axis=0, keepdims=True) * -0.25
+            high, mid, low = split_three(jnp.where(row == 7, square, tile))
+            left = jnp.concatenate([high, high, high, mid, mid, low, minus, zero], axis=0)
+            left = left.astype(jnp.bfloat16).T
+
             slot = code & 511
-            block = code >> 9
             source = jnp.minimum(lax.div(slot, slots), near - 1)
             start = source * (6 * slots) + lax.rem(slot, slots)
             tile = nodes_ref[pl.ds(start, 6, stride=slots), :]
@@ -184,11 +161,7 @@
                 ],
                 axis=1,
             )
-            first = (block & 1) == 0
-            right = jnp.concatenate(
-                [jnp.where(first, right, nothing), jnp.where(first, nothing, right)], axis=0
-            )
-            both = jnp.dot(left_ref[block >> 1], right, preferred_element_type=jnp.float32)
+            both = jnp.dot(left, right, preferred_element_type=jnp.float32)
             pressure = jnp.exp2(both[:, BLK:]) * jnp.maximum(both[:, :BLK], 0.0)
             high = pressure.astype(jnp.bfloat16)
             press[n, 0:BLK] = high
@@ -197,25 +170,33 @@
     def finish(k):
         for n in range(TOGETHER):
             code = todo_ref[k * TOGETHER + n]
-            normal = normal_ref[code >> 9]
+            normal = jnp.concatenate(split_two(geometry(code)), axis=0).astype(jnp.bfloat16)
             normal = jnp.concatenate([normal, normal], axis=1)
             force = jnp.dot(normal, press[n], preferred_element_type=jnp.float32)
             at = pl.ds(pl.multiple_of((code & 511) * 8, 8), 8)
-            total[at, :] = total[at, :] + (force + pltpu.roll(force, 5, 0))
+            total[at, :] = total[at, :] + (force[0:8] + force[8:16])
 
     def step(k, _):
         finish(k)
         begin(k + 1)
         return 0
 
-    steps = lax.div(count_ref[0] + (TOGETHER - 1), TOGETHER)
+    def keep(k, count):
+        code = codes_ref[k]
+        todo_ref[count] = code
+        return count + 1 + (code >> 31)
+
+    count = lax.fori_loop(0, codes_ref.shape[0], keep, jnp.int32(0), unroll=16)
+    for k in range(2 * TOGETHER):
+        todo_ref[count + k] = NOBODY
+    steps = lax.div(count + (TOGETHER - 1), TOGETHER)
     begin(0)
     lax.fori_loop(0, steps, step, 0)
     for source in range(near):
         for comp in range(3):
             for half in range(slots // 8):
                 out_ref[source, comp, half * 8 : half * 8 + 8, :] = total[
-                    pl.ds((source * slots + half * 8) * 8 + comp, 8, stride=8), :
+                    pl.ds((source * slots + half * 8) * 8 + 3 + comp, 8, stride=8), :
                 ]
 
 
@@ -238,7 +219,6 @@
     per_group = pair_seg.shape[2]
     slots = copies * 2
     owners = groups * copies
-    total_blocks = owners * seg_blocks
 
     outgoing, pick, geometry = pl.pallas_call(
         functools.partial(start_kernel, copies, near),
@@ -257,11 +237,14 @@
         pair_seg,
         pair_slot,
     )
+    geometry = geometry.reshape(seg_blocks * 8, BLK)
+    pieces = [geometry]
+    for other in range(1, copies):
+        pieces.append(lax.ppermute(geometry, "zh", [(i, i ^ other) for i in range(copies)]))
     received = lax.all_to_all(
         outgoing.reshape(near, 6 * slots, BLK), NEAR, split_axis=0, concat_axis=0, tiled=True
     )
-    geometry = lax.all_gather(geometry.reshape(seg_blocks * 8, BLK), "zh", axis=0, tiled=True)
-    geometry = lax.all_gather(geometry, "grp", axis=0, tiled=True)
+    geometry = lax.all_gather(jnp.concatenate(pieces, axis=0), "grp", axis=0, tiled=True)
 
     tables = geometry.reshape(owners, seg_blocks, 8, BLK)[:, :, 7, :per_group].astype(jnp.int32)
     row = lax.axis_index("grp")
@@ -269,34 +252,23 @@
     seg = lax.dynamic_index_in_dim(tables, row + groups, axis=1, keepdims=False)
     owner = jnp.arange(owners, dtype=jnp.int32)[:, None]
     source = slot // 2
-    place = (owner % copies) * 2 + slot % 2
+    place = (lax.axis_index("zh") ^ (owner % copies)) * 2 + slot % 2
     block = owner * seg_blocks + seg
     codes = (source % near) * slots + place + block * 512
     codes = jnp.where(source // near == lax.axis_index("zh"), codes, -1).reshape(-1)
 
-    todo, count, left, normal = pl.pallas_call(
-        ready_kernel,
-        out_shape=(
-            jax.ShapeDtypeStruct((codes.shape[0] + 2 * TOGETHER,), jnp.int32),
-            jax.ShapeDtypeStruct((1,), jnp.int32),
-            jax.ShapeDtypeStruct((total_blocks // 2, BLK, BLK), jnp.bfloat16),
-            jax.ShapeDtypeStruct((total_blocks, 8, BLK), jnp.bfloat16),
-        ),
-        in_specs=[SMEM, VMEM],
-        out_specs=[SMEM, SMEM, VMEM, VMEM],
-        compiler_params=room(14),
-    )(codes, geometry.reshape(total_blocks * 8, BLK))
     forces = pl.pallas_call(
         force_kernel,
         out_shape=f32(near, 3, slots, BLK),
-        in_specs=[SMEM, SMEM, VMEM, VMEM, VMEM],
+        in_specs=[SMEM, VMEM, VMEM],
         out_specs=VMEM,
         scratch_shapes=[
             pltpu.VMEM(((near * slots + 1) * 8, BLK), jnp.float32),
             pltpu.VMEM((TOGETHER, 2 * BLK, BLK), jnp.bfloat16),
+            pltpu.SMEM((codes.shape[0] + 2 * TOGETHER,), jnp.int32),
         ],
         compiler_params=room(20),
-    )(todo, count, left, normal, received.reshape(near * 6 * slots, BLK))
+    )(codes, geometry, received.reshape(near * 6 * slots, BLK))
     back = lax.all_to_all(
         forces.reshape(near, 3 * slots, BLK), NEAR, split_axis=0, concat_axis=0, tiled=True
     )

time: 105 us -> 87 us (0.83)
  blocking collectives: 72.4 us -> 36.9 us
  starting transfers between devices: 10.4 us -> 29 us
  waiting for transfers between devices: 0.01 us -> 9.36 us
  Pallas kernels: 19.2 us -> 10.5 us
  local copies, waits for them, and re-layouts: 2.16 us -> 0.52 us
    all_gather x2 -> x1, blocking collectives: 39.6 us -> 11.3 us  [contact(): lax.all_gather(jnp.concatenate(pieces, axis=0), 'grp', axis=0, tiled=True)]
    ppermute x0 -> x3, starting transfers between devices: none -> 18.5 us  [contact(): lax.ppermute(geometry, 'zh', [(i, i ^ other) for i in range(copies)])]
    ppermute x0 -> x3, waiting for transfers between devices: none -> 9.35 us  [contact(): lax.ppermute(geometry, 'zh', [(i, i ^ other) for i in range(copies)])]
    all_to_all x1, blocking collectives: 32.8 us -> 25.6 us  [contact(): lax.all_to_all(forces.reshape(near, 3 * slots, BLK), NEAR, split_axis=0,...]
    pallas_call x1 -> x0, Pallas kernels: 6.53 us -> none  [contact(): pl.pallas_call(ready_kernel, out_shape=(jax.ShapeDtypeStruct((codes.shape...]
    pallas_call x1, Pallas kernels: 9.18 us -> 7.07 us  [contact(): pl.pallas_call(force_kernel, out_shape=f32(near, 3, slots, BLK), in_specs...]
    unnamed x6 -> x4, local copies, waits for them, and re-layouts: 1.65 us -> 0.01 us
  transfers between devices with their start and end apart: 1 -> 4, of which waited for: 0 -> 2; matrix products, arithmetic and copies ran while one was open for 1% -> 1% of each run, Pallas kernels for 6% -> 0%
where the time goes in v4:
time: 87 us; the launch traced here: 86.5 us
  blocking collectives  36.9 us (42%)
  starting transfers between devices  29 us (33%)
  Pallas kernels  10.5 us (12%)
  waiting for transfers between devices  9.36 us (11%)
    all_to_all x1, blocking collectives, contact(): lax.all_to_all(forces.reshape(near, 3 * slots, BLK), NEAR, split_axis=0,...  25.6 us
    ppermute x3, starting transfers between devices, contact(): lax.ppermute(geometry, 'zh', [(i, i ^ other) for i in range(copies)])  18.5 us
    all_gather x1, blocking collectives, contact(): lax.all_gather(jnp.concatenate(pieces, axis=0), 'grp', axis=0, tiled=True)  11.3 us
    all_to_all x1, starting transfers between devices, contact(): lax.all_to_all(outgoing.reshape(near, 6 * slots, BLK), NEAR, split_axis=0...  10.5 us
    ppermute x3, waiting for transfers between devices, contact(): lax.ppermute(geometry, 'zh', [(i, i ^ other) for i in range(copies)])  9.35 us
    pallas_call x1, Pallas kernels, contact(): pl.pallas_call(force_kernel, out_shape=f32(near, 3, slots, BLK), in_specs...  7.07 us
    pallas_call x1, Pallas kernels, contact(): pl.pallas_call(functools.partial(start_kernel, copies, near), out_shape=(...  2.46 us
  transfers between devices with their start and end apart: 4, of which 2 were waited for; matrix products, arithmetic and copies ran while one was open for 1% of the time, Pallas kernels for 0%

profile of v4, /device:TPU:1, one launch (start us, length us, event | category | flops | bytes accessed | tf_op | source)
XLA Modules:
  0.0 86.5 jit_solution(13953694432986174500)
XLA Ops:
  0.0 2.5 %shard_map.64 = (f32[32,6,8,128]{3,2,1,0:T(8,128)}, bf16[128,256]{1,0:T(8,128)(2,1)}, f32[8,8,128]{2,1,0:T(8,128)}) custom-call(s32[1,128]{1,0:T(1,128)} %bitcast.19, f32[6,128,128]{2,1,0:T(8,128)} %bitcast.14, f32[6,512]{1,0:T(8,128)} %corners_ref.1, s32[3,1024]{1,0:T(4,128)} %conn_ref.1, s32[1,4,32]{2,1,0:T(4,128)} %seg_ref.1, s32[1,4,32]{2,1,0:T(4,128)} %slot_ref.1), custom_call_target="tpu_custom_call" | custom-call | tf_op jit(solution)/shard_map/pallas_call | solution.py:223
  2.5 0.0 copy-start.1
  2.5 10.5 %all-to-all-start = ((f32[32,48,128]{2,1,0:T(8,128)}), f32[32,48,128]{2,1,0:T(8,128)S(1)}, u32[]{:S(2)}, u32[]{:S(2)}) async-start(f32[32,48,128]{2,1,0:T(8,128)} %bitcast.13), calls=%async_computation | async-start | bytes 1572864 | tf_op jit(solution)/shard_map/all_to_all | solution.py:244
  13.0 0.0 copy-done.1
  13.0 9.5 %collective-permute-start.2 = (f32[64,128]{1,0:T(8,128)S(1)}, f32[64,128]{1,0:T(8,128)S(1)}, u32[]{:S(2)}, u32[]{:S(2)}) collective-permute-start(f32[64,128]{1,0:T(8,128)S(1)} %bitcast.15), channel_id=1, source_target_pairs={{0,96},{32,64},{64,32},{96,0},{1,97},{33,65},{65,33},{97,1},{2,98}... | collective-permute-start | bytes 98312 | tf_op jit(solution)/shard_map/ppermute | solution.py:243
  22.6 6.1 %collective-permute-start.1 = (f32[64,128]{1,0:T(8,128)S(1)}, f32[64,128]{1,0:T(8,128)S(1)}, u32[]{:S(2)}, u32[]{:S(2)}) collective-permute-start(f32[64,128]{1,0:T(8,128)S(1)} %bitcast.16), channel_id=1, source_target_pairs={{0,64},{32,96},{64,0},{96,32},{1,65},{33,97},{65,1},{97,33},{2,66}... | collective-permute-start | bytes 98312 | tf_op jit(solution)/shard_map/ppermute | solution.py:243
  28.6 2.9 %collective-permute-start = (f32[64,128]{1,0:T(8,128)S(1)}, f32[64,128]{1,0:T(8,128)S(1)}, u32[]{:S(2)}, u32[]{:S(2)}) collective-permute-start(f32[64,128]{1,0:T(8,128)S(1)} %bitcast.17), channel_id=1, source_target_pairs={{0,32},{32,0},{64,96},{96,64},{1,33},{33,1},{65,97},{97,65},{2,34}... | collective-permute-start | bytes 98312 | tf_op jit(solution)/shard_map/ppermute | solution.py:243
  31.5 0.1 add.77
  31.6 0.1 add.78
  31.7 0.1 add.72
  31.8 0.1 add.73
  31.8 3.2 %collective-permute-done.2 = f32[64,128]{1,0:T(8,128)S(1)} collective-permute-done((f32[64,128]{1,0:T(8,128)S(1)}, f32[64,128]{1,0:T(8,128)S(1)}, u32[]{:S(2)}, u32[]{:S(2)}) %collective-permute-start.2) | collective-permute-done | bytes 32800 | tf_op jit(solution)/shard_map/ppermute | solution.py:243
  35.1 6.1 %collective-permute-done.1 = f32[64,128]{1,0:T(8,128)S(1)} collective-permute-done((f32[64,128]{1,0:T(8,128)S(1)}, f32[64,128]{1,0:T(8,128)S(1)}, u32[]{:S(2)}, u32[]{:S(2)}) %collective-permute-start.1) | collective-permute-done | bytes 32800 | tf_op jit(solution)/shard_map/ppermute | solution.py:243
  41.2 0.0 collective-permute-done
  41.2 11.3 %all_gather.3.geo_ref = f32[1024,128]{1,0:T(8,128)S(1)} all-gather(f32[256,128]{1,0:T(8,128)S(1)} %pad_maximum_fusion), channel_id=1, replica_groups=mesh['grp'=4,'zh'=4,'zl'=4,'y'=4,'core'=2] {'grp'}, dimensions={0}, use_global_device_ids=true | all-gather | bytes 655360 | tf_op jit(solution)/shard_map/all_gather | solution.py:247
  52.5 0.1 slice_convert_fusion
  52.6 0.1 dynamic-slice_reduce_fusion.1
  52.7 0.1 squeeze.8
  52.7 0.1 squeeze.9
  52.9 0.0 all-to-all-done
  52.9 7.1 %shard_map.65 = f32[32,3,8,128]{3,2,1,0:T(8,128)S(1)} custom-call(s32[512]{0:T(512)S(1)} %fusion.4.codes_ref, f32[1024,128]{1,0:T(8,128)S(1)} %all_gather.3.geo_ref, f32[1536,128]{1,0:T(8,128)S(1)} %bitcast.9), custom_call_target="tpu_custom_call" | custom-call | tf_op jit(solution)/shard_map/pallas_call | solution.py:260
  59.9 0.0 copy-start
  60.0 25.6 %all_to_all.10 = f32[32,24,128]{2,1,0:T(8,128)S(1)} all-to-all(f32[32,24,128]{2,1,0:T(8,128)S(1)} %bitcast.12), channel_id=1, replica_groups=mesh['grp'=4,'zh'=4,'zl'=4,'y'=4,'core'=2] {'zl','y','core'}, dimensions={0} | all-to-all | bytes 786432 | tf_op jit(solution)/shard_map/all_to_all | solution.py:272
  85.5 0.0 copy-done
  85.6 1.0 %shard_map.66 = f32[3,128,128]{2,1,0:T(8,128)} custom-call(bf16[128,256]{1,0:T(8,128)(2,1)S(1)} %copy-done, f32[32,3,8,128]{3,2,1,0:T(8,128)S(1)} %bitcast.11), custom_call_target="tpu_custom_call" | custom-call | tf_op jit(solution)/shard_map/pallas_call | solution.py:275
  (4 shorter events, 0.0 us)
Async XLA Ops:
  2.5 10.5 %copy-start.1 = (f32[8,8,128]{2,1,0:T(8,128)S(1)}, f32[8,8,128]{2,1,0:T(8,128)}, u32[]{:S(2)}) copy-start(f32[8,8,128]{2,1,0:T(8,128)} %get-tuple-element.9) | copy-start | bytes 98308
  2.5 50.4 %all-to-all-start = ((f32[32,48,128]{2,1,0:T(8,128)}), f32[32,48,128]{2,1,0:T(8,128)S(1)}, u32[]{:S(2)}, u32[]{:S(2)}) async-start(f32[32,48,128]{2,1,0:T(8,128)} %bitcast.13), calls=%async_computation | async-start | bytes 1572864 | tf_op jit(solution)/shard_map/all_to_all | solution.py:244
  13.0 22.1 %collective-permute-start.2 = (f32[64,128]{1,0:T(8,128)S(1)}, f32[64,128]{1,0:T(8,128)S(1)}, u32[]{:S(2)}, u32[]{:S(2)}) collective-permute-start(f32[64,128]{1,0:T(8,128)S(1)} %bitcast.15), channel_id=1, source_target_pairs={{0,96},{32,64},{64,32},{96,0},{1,97},{33,65},{65,33},{97,1},{2,98}... | collective-permute-start | bytes 98312 | tf_op jit(solution)/shard_map/ppermute | solution.py:243
  22.6 18.6 %collective-permute-start.1 = (f32[64,128]{1,0:T(8,128)S(1)}, f32[64,128]{1,0:T(8,128)S(1)}, u32[]{:S(2)}, u32[]{:S(2)}) collective-permute-start(f32[64,128]{1,0:T(8,128)S(1)} %bitcast.16), channel_id=1, source_target_pairs={{0,64},{32,96},{64,0},{96,32},{1,65},{33,97},{65,1},{97,33},{2,66}... | collective-permute-start | bytes 98312 | tf_op jit(solution)/shard_map/ppermute | solution.py:243
  28.6 12.6 %collective-permute-start = (f32[64,128]{1,0:T(8,128)S(1)}, f32[64,128]{1,0:T(8,128)S(1)}, u32[]{:S(2)}, u32[]{:S(2)}) collective-permute-start(f32[64,128]{1,0:T(8,128)S(1)} %bitcast.17), channel_id=1, source_target_pairs={{0,32},{32,0},{64,96},{96,64},{1,33},{33,1},{65,97},{97,65},{2,34}... | collective-permute-start | bytes 98312 | tf_op jit(solution)/shard_map/ppermute | solution.py:243
  59.9 25.6 %copy-start = (bf16[128,256]{1,0:T(8,128)(2,1)S(1)}, bf16[128,256]{1,0:T(8,128)(2,1)}, u32[]{:S(2)}) copy-start(bf16[128,256]{1,0:T(8,128)(2,1)} %get-tuple-element.8.pick_ref) | copy-start | bytes 196612

commit v5 on v4

--- a/solution.py
+++ b/solution.py
@@ -20,7 +20,7 @@
 NEAR = ("zl", "y", "core")
 VMEM = pl.BlockSpec(memory_space=pltpu.VMEM)
 SMEM = pl.BlockSpec(memory_space=pltpu.SMEM)
-TOGETHER = 12
+TOGETHER = 16
 NOBODY = 256
 
 
@@ -186,12 +186,13 @@
         todo_ref[count] = code
         return count + 1 + (code >> 31)
 
-    count = lax.fori_loop(0, codes_ref.shape[0], keep, jnp.int32(0), unroll=16)
+    count = lax.fori_loop(0, codes_ref.shape[0], keep, jnp.int32(0), unroll=64)
     for k in range(2 * TOGETHER):
         todo_ref[count + k] = NOBODY
-    steps = lax.div(count + (TOGETHER - 1), TOGETHER)
+    last = jnp.maximum(lax.div(count + (TOGETHER - 1), TOGETHER) - 1, 0)
     begin(0)
-    lax.fori_loop(0, steps, step, 0)
+    lax.fori_loop(0, last, step, 0)
+    finish(last)
     for source in range(near):
         for comp in range(3):
             for half in range(slots // 8):

time: 87 us -> 86.3 us (level)
  no operation moved by 1% of the time
where the time goes in v5:
time: 86.3 us; the launch traced here: 85.9 us
  blocking collectives  36.6 us (42%)
  starting transfers between devices  29 us (34%)
  Pallas kernels  10.2 us (12%)
  waiting for transfers between devices  9.36 us (11%)
    all_to_all x1, blocking collectives, contact(): lax.all_to_all(forces.reshape(near, 3 * slots, BLK), NEAR, split_axis=0,...  25.2 us
    ppermute x3, starting transfers between devices, contact(): lax.ppermute(geometry, 'zh', [(i, i ^ other) for i in range(copies)])  18.5 us
    all_gather x1, blocking collectives, contact(): lax.all_gather(jnp.concatenate(pieces, axis=0), 'grp', axis=0, tiled=True)  11.3 us
    all_to_all x1, starting transfers between devices, contact(): lax.all_to_all(outgoing.reshape(near, 6 * slots, BLK), NEAR, split_axis=0...  10.5 us
    ppermute x3, waiting for transfers between devices, contact(): lax.ppermute(geometry, 'zh', [(i, i ^ other) for i in range(copies)])  9.35 us
    pallas_call x1, Pallas kernels, contact(): pl.pallas_call(force_kernel, out_shape=f32(near, 3, slots, BLK), in_specs...  6.75 us
    pallas_call x1, Pallas kernels, contact(): pl.pallas_call(functools.partial(start_kernel, copies, near), out_shape=(...  2.46 us
  transfers between devices with their start and end apart: 4, of which 2 were waited for; matrix products, arithmetic and copies ran while one was open for 1% of the time, Pallas kernels for 0%

profile of v5, /device:TPU:1, one launch (start us, length us, event | category | flops | bytes accessed | tf_op | source)
XLA Modules:
  0.0 85.9 jit_solution(5999777038200875175)
XLA Ops:
  0.0 2.5 %shard_map.64 = (f32[32,6,8,128]{3,2,1,0:T(8,128)}, bf16[128,256]{1,0:T(8,128)(2,1)}, f32[8,8,128]{2,1,0:T(8,128)}) custom-call(s32[1,128]{1,0:T(1,128)} %bitcast.19, f32[6,128,128]{2,1,0:T(8,128)} %bitcast.14, f32[6,512]{1,0:T(8,128)} %corners_ref.1, s32[3,1024]{1,0:T(4,128)} %conn_ref.1, s32[1,4,32]{2,1,0:T(4,128)} %seg_ref.1, s32[1,4,32]{2,1,0:T(4,128)} %slot_ref.1), custom_call_target="tpu_custom_call" | custom-call | tf_op jit(solution)/shard_map/pallas_call | solution.py:224
  2.5 0.0 copy-start.1
  2.5 10.5 %all-to-all-start = ((f32[32,48,128]{2,1,0:T(8,128)}), f32[32,48,128]{2,1,0:T(8,128)S(1)}, u32[]{:S(2)}, u32[]{:S(2)}) async-start(f32[32,48,128]{2,1,0:T(8,128)} %bitcast.13), calls=%async_computation | async-start | bytes 1572864 | tf_op jit(solution)/shard_map/all_to_all | solution.py:245
  13.0 0.0 copy-done.1
  13.0 9.5 %collective-permute-start.2 = (f32[64,128]{1,0:T(8,128)S(1)}, f32[64,128]{1,0:T(8,128)S(1)}, u32[]{:S(2)}, u32[]{:S(2)}) collective-permute-start(f32[64,128]{1,0:T(8,128)S(1)} %bitcast.15), channel_id=1, source_target_pairs={{0,96},{32,64},{64,32},{96,0},{1,97},{33,65},{65,33},{97,1},{2,98}... | collective-permute-start | bytes 98312 | tf_op jit(solution)/shard_map/ppermute | solution.py:244
  22.6 6.1 %collective-permute-start.1 = (f32[64,128]{1,0:T(8,128)S(1)}, f32[64,128]{1,0:T(8,128)S(1)}, u32[]{:S(2)}, u32[]{:S(2)}) collective-permute-start(f32[64,128]{1,0:T(8,128)S(1)} %bitcast.16), channel_id=1, source_target_pairs={{0,64},{32,96},{64,0},{96,32},{1,65},{33,97},{65,1},{97,33},{2,66}... | collective-permute-start | bytes 98312 | tf_op jit(solution)/shard_map/ppermute | solution.py:244
  28.6 2.9 %collective-permute-start = (f32[64,128]{1,0:T(8,128)S(1)}, f32[64,128]{1,0:T(8,128)S(1)}, u32[]{:S(2)}, u32[]{:S(2)}) collective-permute-start(f32[64,128]{1,0:T(8,128)S(1)} %bitcast.17), channel_id=1, source_target_pairs={{0,32},{32,0},{64,96},{96,64},{1,33},{33,1},{65,97},{97,65},{2,34}... | collective-permute-start | bytes 98312 | tf_op jit(solution)/shard_map/ppermute | solution.py:244
  31.5 0.1 add.77
  31.6 0.1 add.78
  31.7 0.1 add.72
  31.8 0.1 add.73
  31.8 3.2 %collective-permute-done.2 = f32[64,128]{1,0:T(8,128)S(1)} collective-permute-done((f32[64,128]{1,0:T(8,128)S(1)}, f32[64,128]{1,0:T(8,128)S(1)}, u32[]{:S(2)}, u32[]{:S(2)}) %collective-permute-start.2) | collective-permute-done | bytes 32800 | tf_op jit(solution)/shard_map/ppermute | solution.py:244
  35.1 6.1 %collective-permute-done.1 = f32[64,128]{1,0:T(8,128)S(1)} collective-permute-done((f32[64,128]{1,0:T(8,128)S(1)}, f32[64,128]{1,0:T(8,128)S(1)}, u32[]{:S(2)}, u32[]{:S(2)}) %collective-permute-start.1) | collective-permute-done | bytes 32800 | tf_op jit(solution)/shard_map/ppermute | solution.py:244
  41.2 0.0 collective-permute-done
  41.2 11.3 %all_gather.3.geo_ref = f32[1024,128]{1,0:T(8,128)S(1)} all-gather(f32[256,128]{1,0:T(8,128)S(1)} %pad_maximum_fusion), channel_id=1, replica_groups=mesh['grp'=4,'zh'=4,'zl'=4,'y'=4,'core'=2] {'grp'}, dimensions={0}, use_global_device_ids=true | all-gather | bytes 655360 | tf_op jit(solution)/shard_map/all_gather | solution.py:248
  52.5 0.1 slice_convert_fusion
  52.6 0.1 dynamic-slice_reduce_fusion.1
  52.7 0.1 squeeze.8
  52.7 0.1 squeeze.9
  52.9 0.0 all-to-all-done
  52.9 6.7 %shard_map.65 = f32[32,3,8,128]{3,2,1,0:T(8,128)S(1)} custom-call(s32[512]{0:T(512)S(1)} %fusion.4.codes_ref, f32[1024,128]{1,0:T(8,128)S(1)} %all_gather.3.geo_ref, f32[1536,128]{1,0:T(8,128)S(1)} %bitcast.9), custom_call_target="tpu_custom_call" | custom-call | tf_op jit(solution)/shard_map/pallas_call | solution.py:261
  59.6 0.0 copy-start
  59.6 25.2 %all_to_all.10 = f32[32,24,128]{2,1,0:T(8,128)S(1)} all-to-all(f32[32,24,128]{2,1,0:T(8,128)S(1)} %bitcast.12), channel_id=1, replica_groups=mesh['grp'=4,'zh'=4,'zl'=4,'y'=4,'core'=2] {'zl','y','core'}, dimensions={0} | all-to-all | bytes 786432 | tf_op jit(solution)/shard_map/all_to_all | solution.py:273
  84.9 0.0 copy-done
  84.9 1.0 %shard_map.66 = f32[3,128,128]{2,1,0:T(8,128)} custom-call(bf16[128,256]{1,0:T(8,128)(2,1)S(1)} %copy-done, f32[32,3,8,128]{3,2,1,0:T(8,128)S(1)} %bitcast.11), custom_call_target="tpu_custom_call" | custom-call | tf_op jit(solution)/shard_map/pallas_call | solution.py:276
  (4 shorter events, 0.0 us)
Async XLA Ops:
  2.5 10.5 %copy-start.1 = (f32[8,8,128]{2,1,0:T(8,128)S(1)}, f32[8,8,128]{2,1,0:T(8,128)}, u32[]{:S(2)}) copy-start(f32[8,8,128]{2,1,0:T(8,128)} %get-tuple-element.9) | copy-start | bytes 98308
  2.5 50.4 %all-to-all-start = ((f32[32,48,128]{2,1,0:T(8,128)}), f32[32,48,128]{2,1,0:T(8,128)S(1)}, u32[]{:S(2)}, u32[]{:S(2)}) async-start(f32[32,48,128]{2,1,0:T(8,128)} %bitcast.13), calls=%async_computation | async-start | bytes 1572864 | tf_op jit(solution)/shard_map/all_to_all | solution.py:245
  13.0 22.1 %collective-permute-start.2 = (f32[64,128]{1,0:T(8,128)S(1)}, f32[64,128]{1,0:T(8,128)S(1)}, u32[]{:S(2)}, u32[]{:S(2)}) collective-permute-start(f32[64,128]{1,0:T(8,128)S(1)} %bitcast.15), channel_id=1, source_target_pairs={{0,96},{32,64},{64,32},{96,0},{1,97},{33,65},{65,33},{97,1},{2,98}... | collective-permute-start | bytes 98312 | tf_op jit(solution)/shard_map/ppermute | solution.py:244
  22.6 18.6 %collective-permute-start.1 = (f32[64,128]{1,0:T(8,128)S(1)}, f32[64,128]{1,0:T(8,128)S(1)}, u32[]{:S(2)}, u32[]{:S(2)}) collective-permute-start(f32[64,128]{1,0:T(8,128)S(1)} %bitcast.16), channel_id=1, source_target_pairs={{0,64},{32,96},{64,0},{96,32},{1,65},{33,97},{65,1},{97,33},{2,66}... | collective-permute-start | bytes 98312 | tf_op jit(solution)/shard_map/ppermute | solution.py:244
  28.6 12.6 %collective-permute-start = (f32[64,128]{1,0:T(8,128)S(1)}, f32[64,128]{1,0:T(8,128)S(1)}, u32[]{:S(2)}, u32[]{:S(2)}) collective-permute-start(f32[64,128]{1,0:T(8,128)S(1)} %bitcast.17), channel_id=1, source_target_pairs={{0,32},{32,0},{64,96},{96,64},{1,33},{33,1},{65,97},{97,65},{2,34}... | collective-permute-start | bytes 98312 | tf_op jit(solution)/shard_map/ppermute | solution.py:244
  59.6 25.2 %copy-start = (bf16[128,256]{1,0:T(8,128)(2,1)S(1)}, bf16[128,256]{1,0:T(8,128)(2,1)}, u32[]{:S(2)}) copy-start(bf16[128,256]{1,0:T(8,128)(2,1)} %get-tuple-element.8.pick_ref) | copy-start | bytes 196612

commit v6 on v5

--- a/solution.py
+++ b/solution.py
@@ -120,7 +120,19 @@
     return high, mid, low
 
 
-def force_kernel(codes_ref, geo_ref, nodes_ref, out_ref, total, press, todo_ref):
+def list_kernel(codes_ref, todo_ref, count_ref):
+    def keep(k, count):
+        code = codes_ref[k]
+        todo_ref[count] = code
+        return count + 1 + (code >> 31)
+
+    count = lax.fori_loop(0, codes_ref.shape[0], keep, jnp.int32(0), unroll=64)
+    for k in range(2 * TOGETHER):
+        todo_ref[count + k] = NOBODY
+    count_ref[0] = count
+
+
+def force_kernel(todo_ref, count_ref, geo_ref, nodes_ref, out_ref, total, press):
     near, _, slots, _ = out_ref.shape
     total[...] = jnp.zeros_like(total)
     row = lax.broadcasted_iota(jnp.int32, (8, BLK), 0)
@@ -181,15 +193,7 @@
         begin(k + 1)
         return 0
 
-    def keep(k, count):
-        code = codes_ref[k]
-        todo_ref[count] = code
-        return count + 1 + (code >> 31)
-
-    count = lax.fori_loop(0, codes_ref.shape[0], keep, jnp.int32(0), unroll=64)
-    for k in range(2 * TOGETHER):
-        todo_ref[count + k] = NOBODY
-    last = jnp.maximum(lax.div(count + (TOGETHER - 1), TOGETHER) - 1, 0)
+    last = jnp.maximum(lax.div(count_ref[0] + (TOGETHER - 1), TOGETHER) - 1, 0)
     begin(0)
     lax.fori_loop(0, last, step, 0)
     finish(last)
@@ -258,18 +262,27 @@
     codes = (source % near) * slots + place + block * 512
     codes = jnp.where(source // near == lax.axis_index("zh"), codes, -1).reshape(-1)
 
+    todo, count = pl.pallas_call(
+        list_kernel,
+        out_shape=(
+            jax.ShapeDtypeStruct((codes.shape[0] + 2 * TOGETHER,), jnp.int32),
+            jax.ShapeDtypeStruct((1,), jnp.int32),
+        ),
+        in_specs=[SMEM],
+        out_specs=[SMEM, SMEM],
+        compiler_params=room(1),
+    )(codes)
     forces = pl.pallas_call(
         force_kernel,
         out_shape=f32(near, 3, slots, BLK),
-        in_specs=[SMEM, VMEM, VMEM],
+        in_specs=[SMEM, SMEM, VMEM, VMEM],
         out_specs=VMEM,
         scratch_shapes=[
             pltpu.VMEM(((near * slots + 1) * 8, BLK), jnp.float32),
             pltpu.VMEM((TOGETHER, 2 * BLK, BLK), jnp.bfloat16),
-            pltpu.SMEM((codes.shape[0] + 2 * TOGETHER,), jnp.int32),
         ],
         compiler_params=room(20),
-    )(codes, geometry, received.reshape(near * 6 * slots, BLK))
+    )(todo, count, geometry, received.reshape(near * 6 * slots, BLK))
     back = lax.all_to_all(
         forces.reshape(near, 3 * slots, BLK), NEAR, split_axis=0, concat_axis=0, tiled=True
     )

time: 86.3 us -> 88 us (1.020)
  Pallas kernels: 10.2 us -> 12 us
    pallas_call x0 -> x1, Pallas kernels: none -> 2.46 us  [contact(): pl.pallas_call(list_kernel, out_shape=(jax.ShapeDtypeStruct((codes.shape[...]
  transfers between devices with their start and end apart: 4 -> 4, of which waited for: 2 -> 2; matrix products, arithmetic and copies ran while one was open for 1% -> 1% of each run, Pallas kernels for 0% -> 3%
where the time goes in v6:
time: 88 us; the launch traced here: 87.6 us
  blocking collectives  36.6 us (42%)
  starting transfers between devices  29 us (33%)
  Pallas kernels  12 us (14%)
  waiting for transfers between devices  9.36 us (11%)
    all_to_all x1, blocking collectives, contact(): lax.all_to_all(forces.reshape(near, 3 * slots, BLK), NEAR, split_axis=0,...  25.2 us
    ppermute x3, starting transfers between devices, contact(): lax.ppermute(geometry, 'zh', [(i, i ^ other) for i in range(copies)])  18.5 us
    all_gather x1, blocking collectives, contact(): lax.all_gather(jnp.concatenate(pieces, axis=0), 'grp', axis=0, tiled=True)  11.3 us
    all_to_all x1, starting transfers between devices, contact(): lax.all_to_all(outgoing.reshape(near, 6 * slots, BLK), NEAR, split_axis=0...  10.5 us
    ppermute x3, waiting for transfers between devices, contact(): lax.ppermute(geometry, 'zh', [(i, i ^ other) for i in range(copies)])  9.35 us
    pallas_call x1, Pallas kernels, contact(): pl.pallas_call(force_kernel, out_shape=f32(near, 3, slots, BLK), in_specs...  6.03 us
    pallas_call x1, Pallas kernels, contact(): pl.pallas_call(list_kernel, out_shape=(jax.ShapeDtypeStruct((codes.shape[...  2.46 us
    pallas_call x1, Pallas kernels, contact(): pl.pallas_call(functools.partial(start_kernel, copies, near), out_shape=(...  2.46 us
  transfers between devices with their start and end apart: 4, of which 2 were waited for; matrix products, arithmetic and copies ran while one was open for 1% of the time, Pallas kernels for 3%

profile of v6, /device:TPU:1, one launch (start us, length us, event | category | flops | bytes accessed | tf_op | source)
XLA Modules:
  0.0 87.6 jit_solution(16834817553646655121)
XLA Ops:
  0.0 2.5 %shard_map.64 = (f32[32,6,8,128]{3,2,1,0:T(8,128)}, bf16[128,256]{1,0:T(8,128)(2,1)}, f32[8,8,128]{2,1,0:T(8,128)}) custom-call(s32[1,128]{1,0:T(1,128)} %bitcast.19, f32[6,128,128]{2,1,0:T(8,128)} %bitcast.14, f32[6,512]{1,0:T(8,128)} %corners_ref.1, s32[3,1024]{1,0:T(4,128)} %conn_ref.1, s32[1,4,32]{2,1,0:T(4,128)} %seg_ref.1, s32[1,4,32]{2,1,0:T(4,128)} %slot_ref.1), custom_call_target="tpu_custom_call" | custom-call | tf_op jit(solution)/shard_map/pallas_call | solution.py:228
  2.5 0.0 copy-start.1
  2.5 10.5 %all-to-all-start = ((f32[32,48,128]{2,1,0:T(8,128)}), f32[32,48,128]{2,1,0:T(8,128)S(1)}, u32[]{:S(2)}, u32[]{:S(2)}) async-start(f32[32,48,128]{2,1,0:T(8,128)} %bitcast.13), calls=%async_computation | async-start | bytes 1572864 | tf_op jit(solution)/shard_map/all_to_all | solution.py:249
  13.0 0.0 copy-done.1
  13.0 9.5 %collective-permute-start.2 = (f32[64,128]{1,0:T(8,128)S(1)}, f32[64,128]{1,0:T(8,128)S(1)}, u32[]{:S(2)}, u32[]{:S(2)}) collective-permute-start(f32[64,128]{1,0:T(8,128)S(1)} %bitcast.15), channel_id=1, source_target_pairs={{0,96},{32,64},{64,32},{96,0},{1,97},{33,65},{65,33},{97,1},{2,98}... | collective-permute-start | bytes 98312 | tf_op jit(solution)/shard_map/ppermute | solution.py:248
  22.6 6.1 %collective-permute-start.1 = (f32[64,128]{1,0:T(8,128)S(1)}, f32[64,128]{1,0:T(8,128)S(1)}, u32[]{:S(2)}, u32[]{:S(2)}) collective-permute-start(f32[64,128]{1,0:T(8,128)S(1)} %bitcast.16), channel_id=1, source_target_pairs={{0,64},{32,96},{64,0},{96,32},{1,65},{33,97},{65,1},{97,33},{2,66}... | collective-permute-start | bytes 98312 | tf_op jit(solution)/shard_map/ppermute | solution.py:248
  28.6 2.9 %collective-permute-start = (f32[64,128]{1,0:T(8,128)S(1)}, f32[64,128]{1,0:T(8,128)S(1)}, u32[]{:S(2)}, u32[]{:S(2)}) collective-permute-start(f32[64,128]{1,0:T(8,128)S(1)} %bitcast.17), channel_id=1, source_target_pairs={{0,32},{32,0},{64,96},{96,64},{1,33},{33,1},{65,97},{97,65},{2,34}... | collective-permute-start | bytes 98312 | tf_op jit(solution)/shard_map/ppermute | solution.py:248
  31.5 0.1 add.77
  31.6 0.1 add.78
  31.7 0.1 add.72
  31.8 0.1 add.73
  31.8 3.2 %collective-permute-done.2 = f32[64,128]{1,0:T(8,128)S(1)} collective-permute-done((f32[64,128]{1,0:T(8,128)S(1)}, f32[64,128]{1,0:T(8,128)S(1)}, u32[]{:S(2)}, u32[]{:S(2)}) %collective-permute-start.2) | collective-permute-done | bytes 32800 | tf_op jit(solution)/shard_map/ppermute | solution.py:248
  35.1 6.1 %collective-permute-done.1 = f32[64,128]{1,0:T(8,128)S(1)} collective-permute-done((f32[64,128]{1,0:T(8,128)S(1)}, f32[64,128]{1,0:T(8,128)S(1)}, u32[]{:S(2)}, u32[]{:S(2)}) %collective-permute-start.1) | collective-permute-done | bytes 32800 | tf_op jit(solution)/shard_map/ppermute | solution.py:248
  41.2 0.0 collective-permute-done
  41.2 11.3 %all_gather.3.geo_ref = f32[1024,128]{1,0:T(8,128)S(1)} all-gather(f32[256,128]{1,0:T(8,128)S(1)} %pad_maximum_fusion), channel_id=1, replica_groups=mesh['grp'=4,'zh'=4,'zl'=4,'y'=4,'core'=2] {'grp'}, dimensions={0}, use_global_device_ids=true | all-gather | bytes 655360 | tf_op jit(solution)/shard_map/all_gather | solution.py:252
  52.5 0.1 slice_convert_fusion
  52.6 0.1 dynamic-slice_reduce_fusion.1
  52.7 0.1 squeeze.8
  52.7 0.1 squeeze.9
  52.9 2.5 %shard_map.65 = (s32[544]{0:T(1024)S(1)}, s32[1]{0:T(128)}) custom-call(s32[512]{0:T(512)S(1)} %fusion.4.codes_ref), custom_call_target="tpu_custom_call" | custom-call | tf_op jit(solution)/shard_map/pallas_call | solution.py:265
  55.3 0.0 all-to-all-done
  55.3 6.0 %shard_map.66 = f32[32,3,8,128]{3,2,1,0:T(8,128)S(1)} custom-call(s32[544]{0:T(1024)S(1)} %get-tuple-element.12.todo_ref, s32[1]{0:T(128)} %get-tuple-element.13.count_ref, f32[1024,128]{1,0:T(8,128)S(1)} %all_gather.3.geo_ref, f32[1536,128]{1,0:T(8,128)S(1)} %bitcast.9), custom_call_target="tpu_custom_call" | custom-call | tf_op jit(solution)/shard_map/pallas_call | solution.py:275
  61.4 0.0 copy-start
  61.4 25.2 %all_to_all.10 = f32[32,24,128]{2,1,0:T(8,128)S(1)} all-to-all(f32[32,24,128]{2,1,0:T(8,128)S(1)} %bitcast.12), channel_id=1, replica_groups=mesh['grp'=4,'zh'=4,'zl'=4,'y'=4,'core'=2] {'zl','y','core'}, dimensions={0} | all-to-all | bytes 786432 | tf_op jit(solution)/shard_map/all_to_all | solution.py:286
  86.6 0.0 copy-done
  86.6 1.0 %shard_map.67 = f32[3,128,128]{2,1,0:T(8,128)} custom-call(bf16[128,256]{1,0:T(8,128)(2,1)S(1)} %copy-done, f32[32,3,8,128]{3,2,1,0:T(8,128)S(1)} %bitcast.11), custom_call_target="tpu_custom_call" | custom-call | tf_op jit(solution)/shard_map/pallas_call | solution.py:289
  (4 shorter events, 0.0 us)
Async XLA Ops:
  2.5 10.5 %copy-start.1 = (f32[8,8,128]{2,1,0:T(8,128)S(1)}, f32[8,8,128]{2,1,0:T(8,128)}, u32[]{:S(2)}) copy-start(f32[8,8,128]{2,1,0:T(8,128)} %get-tuple-element.11) | copy-start | bytes 98308
  2.5 52.9 %all-to-all-start = ((f32[32,48,128]{2,1,0:T(8,128)}), f32[32,48,128]{2,1,0:T(8,128)S(1)}, u32[]{:S(2)}, u32[]{:S(2)}) async-start(f32[32,48,128]{2,1,0:T(8,128)} %bitcast.13), calls=%async_computation | async-start | bytes 1572864 | tf_op jit(solution)/shard_map/all_to_all | solution.py:249
  13.0 22.1 %collective-permute-start.2 = (f32[64,128]{1,0:T(8,128)S(1)}, f32[64,128]{1,0:T(8,128)S(1)}, u32[]{:S(2)}, u32[]{:S(2)}) collective-permute-start(f32[64,128]{1,0:T(8,128)S(1)} %bitcast.15), channel_id=1, source_target_pairs={{0,96},{32,64},{64,32},{96,0},{1,97},{33,65},{65,33},{97,1},{2,98}... | collective-permute-start | bytes 98312 | tf_op jit(solution)/shard_map/ppermute | solution.py:248
  22.6 18.6 %collective-permute-start.1 = (f32[64,128]{1,0:T(8,128)S(1)}, f32[64,128]{1,0:T(8,128)S(1)}, u32[]{:S(2)}, u32[]{:S(2)}) collective-permute-start(f32[64,128]{1,0:T(8,128)S(1)} %bitcast.16), channel_id=1, source_target_pairs={{0,64},{32,96},{64,0},{96,32},{1,65},{33,97},{65,1},{97,33},{2,66}... | collective-permute-start | bytes 98312 | tf_op jit(solution)/shard_map/ppermute | solution.py:248
  28.6 12.6 %collective-permute-start = (f32[64,128]{1,0:T(8,128)S(1)}, f32[64,128]{1,0:T(8,128)S(1)}, u32[]{:S(2)}, u32[]{:S(2)}) collective-permute-start(f32[64,128]{1,0:T(8,128)S(1)} %bitcast.17), channel_id=1, source_target_pairs={{0,32},{32,0},{64,96},{96,64},{1,33},{33,1},{65,97},{97,65},{2,34}... | collective-permute-start | bytes 98312 | tf_op jit(solution)/shard_map/ppermute | solution.py:248
  61.4 25.2 %copy-start = (bf16[128,256]{1,0:T(8,128)(2,1)S(1)}, bf16[128,256]{1,0:T(8,128)(2,1)}, u32[]{:S(2)}) copy-start(bf16[128,256]{1,0:T(8,128)(2,1)} %get-tuple-element.10.pick_ref) | copy-start | bytes 196612

commit v7 on v6

--- a/solution.py
+++ b/solution.py
@@ -120,7 +120,7 @@
     return high, mid, low
 
 
-def list_kernel(codes_ref, todo_ref, count_ref):
+def list_kernel(codes_ref, todo_ref):
     def keep(k, count):
         code = codes_ref[k]
         todo_ref[count] = code
@@ -129,10 +129,10 @@
     count = lax.fori_loop(0, codes_ref.shape[0], keep, jnp.int32(0), unroll=64)
     for k in range(2 * TOGETHER):
         todo_ref[count + k] = NOBODY
-    count_ref[0] = count
-
-
-def force_kernel(todo_ref, count_ref, geo_ref, nodes_ref, out_ref, total, press):
+    todo_ref[todo_ref.shape[0] - 1] = count
+
+
+def force_kernel(todo_ref, geo_ref, nodes_ref, out_ref, total, press):
     near, _, slots, _ = out_ref.shape
     total[...] = jnp.zeros_like(total)
     row = lax.broadcasted_iota(jnp.int32, (8, BLK), 0)
@@ -193,7 +193,7 @@
         begin(k + 1)
         return 0
 
-    last = jnp.maximum(lax.div(count_ref[0] + (TOGETHER - 1), TOGETHER) - 1, 0)
+    last = jnp.maximum(lax.div(todo_ref[todo_ref.shape[0] - 1] + (TOGETHER - 1), TOGETHER) - 1, 0)
     begin(0)
     lax.fori_loop(0, last, step, 0)
     finish(last)
@@ -262,27 +262,24 @@
     codes = (source % near) * slots + place + block * 512
     codes = jnp.where(source // near == lax.axis_index("zh"), codes, -1).reshape(-1)
 
-    todo, count = pl.pallas_call(
+    todo = pl.pallas_call(
         list_kernel,
-        out_shape=(
-            jax.ShapeDtypeStruct((codes.shape[0] + 2 * TOGETHER,), jnp.int32),
-            jax.ShapeDtypeStruct((1,), jnp.int32),
-        ),
+        out_shape=jax.ShapeDtypeStruct((codes.shape[0] + 2 * TOGETHER + 1,), jnp.int32),
         in_specs=[SMEM],
-        out_specs=[SMEM, SMEM],
+        out_specs=SMEM,
         compiler_params=room(1),
     )(codes)
     forces = pl.pallas_call(
         force_kernel,
         out_shape=f32(near, 3, slots, BLK),
-        in_specs=[SMEM, SMEM, VMEM, VMEM],
+        in_specs=[SMEM, VMEM, VMEM],
         out_specs=VMEM,
         scratch_shapes=[
             pltpu.VMEM(((near * slots + 1) * 8, BLK), jnp.float32),
             pltpu.VMEM((TOGETHER, 2 * BLK, BLK), jnp.bfloat16),
         ],
         compiler_params=room(20),
-    )(todo, count, geometry, received.reshape(near * 6 * slots, BLK))
+    )(todo, geometry, received.reshape(near * 6 * slots, BLK))
     back = lax.all_to_all(
         forces.reshape(near, 3 * slots, BLK), NEAR, split_axis=0, concat_axis=0, tiled=True
     )

time: 88 us -> 87.4 us (level)
  no operation moved by 1% of the time
where the time goes in v7:
time: 87.4 us; the launch traced here: 87 us
  blocking collectives  36.6 us (42%)
  starting transfers between devices  29 us (33%)
  Pallas kernels  11.3 us (13%)
  waiting for transfers between devices  9.36 us (11%)
    all_to_all x1, blocking collectives, contact(): lax.all_to_all(forces.reshape(near, 3 * slots, BLK), NEAR, split_axis=0,...  25.2 us
    ppermute x3, starting transfers between devices, contact(): lax.ppermute(geometry, 'zh', [(i, i ^ other) for i in range(copies)])  18.5 us
    all_gather x1, blocking collectives, contact(): lax.all_gather(jnp.concatenate(pieces, axis=0), 'grp', axis=0, tiled=True)  11.3 us
    all_to_all x1, starting transfers between devices, contact(): lax.all_to_all(outgoing.reshape(near, 6 * slots, BLK), NEAR, split_axis=0...  10.5 us
    ppermute x3, waiting for transfers between devices, contact(): lax.ppermute(geometry, 'zh', [(i, i ^ other) for i in range(copies)])  9.35 us
    pallas_call x1, Pallas kernels, contact(): pl.pallas_call(force_kernel, out_shape=f32(near, 3, slots, BLK), in_specs...  5.43 us
    pallas_call x1, Pallas kernels, contact(): pl.pallas_call(functools.partial(start_kernel, copies, near), out_shape=(...  2.46 us
    pallas_call x1, Pallas kernels, contact(): pl.pallas_call(list_kernel, out_shape=jax.ShapeDtypeStruct((codes.shape[0...  2.46 us
  transfers between devices with their start and end apart: 4, of which 2 were waited for; matrix products, arithmetic and copies ran while one was open for 1% of the time, Pallas kernels for 3%

profile of v7, /device:TPU:1, one launch (start us, length us, event | category | flops | bytes accessed | tf_op | source)
XLA Modules:
  0.0 87.0 jit_solution(4841842951772297001)
XLA Ops:
  0.0 2.5 %shard_map.64 = (f32[32,6,8,128]{3,2,1,0:T(8,128)}, bf16[128,256]{1,0:T(8,128)(2,1)}, f32[8,8,128]{2,1,0:T(8,128)}) custom-call(s32[1,128]{1,0:T(1,128)} %bitcast.19, f32[6,128,128]{2,1,0:T(8,128)} %bitcast.14, f32[6,512]{1,0:T(8,128)} %corners_ref.1, s32[3,1024]{1,0:T(4,128)} %conn_ref.1, s32[1,4,32]{2,1,0:T(4,128)} %seg_ref.1, s32[1,4,32]{2,1,0:T(4,128)} %slot_ref.1), custom_call_target="tpu_custom_call" | custom-call | tf_op jit(solution)/shard_map/pallas_call | solution.py:228
  2.5 0.0 copy-start.1
  2.5 10.5 %all-to-all-start = ((f32[32,48,128]{2,1,0:T(8,128)}), f32[32,48,128]{2,1,0:T(8,128)S(1)}, u32[]{:S(2)}, u32[]{:S(2)}) async-start(f32[32,48,128]{2,1,0:T(8,128)} %bitcast.13), calls=%async_computation | async-start | bytes 1572864 | tf_op jit(solution)/shard_map/all_to_all | solution.py:249
  13.0 0.0 copy-done.1
  13.0 9.5 %collective-permute-start.2 = (f32[64,128]{1,0:T(8,128)S(1)}, f32[64,128]{1,0:T(8,128)S(1)}, u32[]{:S(2)}, u32[]{:S(2)}) collective-permute-start(f32[64,128]{1,0:T(8,128)S(1)} %bitcast.15), channel_id=1, source_target_pairs={{0,96},{32,64},{64,32},{96,0},{1,97},{33,65},{65,33},{97,1},{2,98}... | collective-permute-start | bytes 98312 | tf_op jit(solution)/shard_map/ppermute | solution.py:248
  22.6 6.1 %collective-permute-start.1 = (f32[64,128]{1,0:T(8,128)S(1)}, f32[64,128]{1,0:T(8,128)S(1)}, u32[]{:S(2)}, u32[]{:S(2)}) collective-permute-start(f32[64,128]{1,0:T(8,128)S(1)} %bitcast.16), channel_id=1, source_target_pairs={{0,64},{32,96},{64,0},{96,32},{1,65},{33,97},{65,1},{97,33},{2,66}... | collective-permute-start | bytes 98312 | tf_op jit(solution)/shard_map/ppermute | solution.py:248
  28.6 2.9 %collective-permute-start = (f32[64,128]{1,0:T(8,128)S(1)}, f32[64,128]{1,0:T(8,128)S(1)}, u32[]{:S(2)}, u32[]{:S(2)}) collective-permute-start(f32[64,128]{1,0:T(8,128)S(1)} %bitcast.17), channel_id=1, source_target_pairs={{0,32},{32,0},{64,96},{96,64},{1,33},{33,1},{65,97},{97,65},{2,34}... | collective-permute-start | bytes 98312 | tf_op jit(solution)/shard_map/ppermute | solution.py:248
  31.5 0.1 add.77
  31.6 0.1 add.78
  31.7 0.1 add.72
  31.8 0.1 add.73
  31.8 3.2 %collective-permute-done.2 = f32[64,128]{1,0:T(8,128)S(1)} collective-permute-done((f32[64,128]{1,0:T(8,128)S(1)}, f32[64,128]{1,0:T(8,128)S(1)}, u32[]{:S(2)}, u32[]{:S(2)}) %collective-permute-start.2) | collective-permute-done | bytes 32800 | tf_op jit(solution)/shard_map/ppermute | solution.py:248
  35.1 6.1 %collective-permute-done.1 = f32[64,128]{1,0:T(8,128)S(1)} collective-permute-done((f32[64,128]{1,0:T(8,128)S(1)}, f32[64,128]{1,0:T(8,128)S(1)}, u32[]{:S(2)}, u32[]{:S(2)}) %collective-permute-start.1) | collective-permute-done | bytes 32800 | tf_op jit(solution)/shard_map/ppermute | solution.py:248
  41.2 0.0 collective-permute-done
  41.2 11.3 %all_gather.3.geo_ref = f32[1024,128]{1,0:T(8,128)S(1)} all-gather(f32[256,128]{1,0:T(8,128)S(1)} %pad_maximum_fusion), channel_id=1, replica_groups=mesh['grp'=4,'zh'=4,'zl'=4,'y'=4,'core'=2] {'grp'}, dimensions={0}, use_global_device_ids=true | all-gather | bytes 655360 | tf_op jit(solution)/shard_map/all_gather | solution.py:252
  52.5 0.1 slice_convert_fusion
  52.6 0.1 dynamic-slice_reduce_fusion.1
  52.7 0.1 squeeze.8
  52.7 0.1 squeeze.9
  52.9 2.5 %shard_map.65.todo_ref = s32[545]{0:T(1024)S(1)} custom-call(s32[512]{0:T(512)S(1)} %fusion.4.codes_ref), custom_call_target="tpu_custom_call" | custom-call | tf_op jit(solution)/shard_map/pallas_call | solution.py:265
  55.3 0.0 all-to-all-done
  55.3 5.4 %shard_map.66 = f32[32,3,8,128]{3,2,1,0:T(8,128)S(1)} custom-call(s32[545]{0:T(1024)S(1)} %shard_map.65.todo_ref, f32[1024,128]{1,0:T(8,128)S(1)} %all_gather.3.geo_ref, f32[1536,128]{1,0:T(8,128)S(1)} %bitcast.9), custom_call_target="tpu_custom_call" | custom-call | tf_op jit(solution)/shard_map/pallas_call | solution.py:272
  60.8 0.0 copy-start
  60.8 25.2 %all_to_all.10 = f32[32,24,128]{2,1,0:T(8,128)S(1)} all-to-all(f32[32,24,128]{2,1,0:T(8,128)S(1)} %bitcast.12), channel_id=1, replica_groups=mesh['grp'=4,'zh'=4,'zl'=4,'y'=4,'core'=2] {'zl','y','core'}, dimensions={0} | all-to-all | bytes 786432 | tf_op jit(solution)/shard_map/all_to_all | solution.py:283
  86.0 0.0 copy-done
  86.0 1.0 %shard_map.67 = f32[3,128,128]{2,1,0:T(8,128)} custom-call(bf16[128,256]{1,0:T(8,128)(2,1)S(1)} %copy-done, f32[32,3,8,128]{3,2,1,0:T(8,128)S(1)} %bitcast.11), custom_call_target="tpu_custom_call" | custom-call | tf_op jit(solution)/shard_map/pallas_call | solution.py:286
  (4 shorter events, 0.0 us)
Async XLA Ops:
  2.5 10.5 %copy-start.1 = (f32[8,8,128]{2,1,0:T(8,128)S(1)}, f32[8,8,128]{2,1,0:T(8,128)}, u32[]{:S(2)}) copy-start(f32[8,8,128]{2,1,0:T(8,128)} %get-tuple-element.9) | copy-start | bytes 98308
  2.5 52.9 %all-to-all-start = ((f32[32,48,128]{2,1,0:T(8,128)}), f32[32,48,128]{2,1,0:T(8,128)S(1)}, u32[]{:S(2)}, u32[]{:S(2)}) async-start(f32[32,48,128]{2,1,0:T(8,128)} %bitcast.13), calls=%async_computation | async-start | bytes 1572864 | tf_op jit(solution)/shard_map/all_to_all | solution.py:249
  13.0 22.1 %collective-permute-start.2 = (f32[64,128]{1,0:T(8,128)S(1)}, f32[64,128]{1,0:T(8,128)S(1)}, u32[]{:S(2)}, u32[]{:S(2)}) collective-permute-start(f32[64,128]{1,0:T(8,128)S(1)} %bitcast.15), channel_id=1, source_target_pairs={{0,96},{32,64},{64,32},{96,0},{1,97},{33,65},{65,33},{97,1},{2,98}... | collective-permute-start | bytes 98312 | tf_op jit(solution)/shard_map/ppermute | solution.py:248
  22.6 18.6 %collective-permute-start.1 = (f32[64,128]{1,0:T(8,128)S(1)}, f32[64,128]{1,0:T(8,128)S(1)}, u32[]{:S(2)}, u32[]{:S(2)}) collective-permute-start(f32[64,128]{1,0:T(8,128)S(1)} %bitcast.16), channel_id=1, source_target_pairs={{0,64},{32,96},{64,0},{96,32},{1,65},{33,97},{65,1},{97,33},{2,66}... | collective-permute-start | bytes 98312 | tf_op jit(solution)/shard_map/ppermute | solution.py:248
  28.6 12.6 %collective-permute-start = (f32[64,128]{1,0:T(8,128)S(1)}, f32[64,128]{1,0:T(8,128)S(1)}, u32[]{:S(2)}, u32[]{:S(2)}) collective-permute-start(f32[64,128]{1,0:T(8,128)S(1)} %bitcast.17), channel_id=1, source_target_pairs={{0,32},{32,0},{64,96},{96,64},{1,33},{33,1},{65,97},{97,65},{2,34}... | collective-permute-start | bytes 98312 | tf_op jit(solution)/shard_map/ppermute | solution.py:248
  60.8 25.3 %copy-start = (bf16[128,256]{1,0:T(8,128)(2,1)S(1)}, bf16[128,256]{1,0:T(8,128)(2,1)}, u32[]{:S(2)}) copy-start(bf16[128,256]{1,0:T(8,128)(2,1)} %get-tuple-element.8.pick_ref) | copy-start | bytes 196612
